TPU v7x, 8 devices: a whole 2x2x1 slice. The times are simulated.
8 devices in a mesh: dp: 1 (over z), fsdp: 8 (over y, x, core).
Axes of the slice: x: 2, y: 2, z: 1, core: 2. Of those that a mesh axis runs over, the one named last changes fastest.
Arguments:
- hidden: bfloat16 [8, 128, 3072], P(('dp', 'fsdp'))
- attn_norm: bfloat16 [2, 3072], P(None, 'fsdp')
- w_q: bfloat16 [2, 3072, 24, 128], P(None, 'fsdp')
- w_k: bfloat16 [2, 3072, 8, 128], P(None, 'fsdp')
- w_v: bfloat16 [2, 3072, 8, 128], P(None, 'fsdp')
- w_o: bfloat16 [2, 3072, 3072], P(None, 'fsdp')
- mlp_norm: bfloat16 [2, 3072], P(None, 'fsdp')
- w_gate: bfloat16 [2, 3072, 8192], P(None, 'fsdp')
- w_up: bfloat16 [2, 3072, 8192], P(None, 'fsdp')
- w_down: bfloat16 [2, 8192, 3072], P(None, 'fsdp')
Outputs:
- output: bfloat16 [8, 128, 3072], P(('dp', 'fsdp'))
All inputs are finite; a program needn't handle non-finite values.
Results may differ from a plain program's by a relative error of at most 0.02.
Values are sent between devices in bfloat16 or wider.
A program may use at most 1 GiB of HBM per device.

v0:
```python
import jax
import jax.numpy as jnp
from jax import lax
from jax.sharding import PartitionSpec as P

ROPE_THETA = 500000.0
NORM_EPS = 1e-5


def rms_norm(hidden, gain):
    wide_hidden = hidden.astype(jnp.float32)
    inv_rms = lax.rsqrt(jnp.mean(wide_hidden * wide_hidden, axis=-1, keepdims=True) + NORM_EPS)
    return (wide_hidden * inv_rms * gain.astype(jnp.float32)).astype(jnp.bfloat16)


def rope_tables(seq_len, head_dim):
    half = head_dim // 2
    inv_freq = jnp.power(ROPE_THETA, -(jnp.arange(half, dtype=jnp.float32) * 2.0 / head_dim))
    angles = jnp.arange(seq_len, dtype=jnp.float32)[:, None] * inv_freq[None, :]
    return jnp.cos(angles)[:, None, :], jnp.sin(angles)[:, None, :]


def apply_rope(proj, cos_table, sin_table):
    half = proj.shape[-1] // 2
    first = proj[..., :half]
    second = proj[..., half:]
    rotated = jnp.concatenate([first * cos_table - second * sin_table, second * cos_table + first * sin_table], axis=-1)
    return rotated.astype(jnp.bfloat16)


def decoder_layer(hidden, attn_gain, w_q, w_k, w_v, w_o, mlp_gain, w_gate, w_up, w_down):
    batch, seq_len = hidden.shape[0], hidden.shape[1]
    heads, head_dim = w_q.shape[1], w_q.shape[2]
    kv_heads = w_k.shape[1]
    group = heads // kv_heads
    cos_table, sin_table = rope_tables(seq_len, head_dim)
    normed = rms_norm(hidden, attn_gain)
    queries = apply_rope(jnp.einsum("bsd,dhe->bshe", normed, w_q, preferred_element_type=jnp.float32), cos_table, sin_table)
    keys_rot = apply_rope(jnp.einsum("bsd,dhe->bshe", normed, w_k, preferred_element_type=jnp.float32), cos_table, sin_table)
    values = jnp.einsum("bsd,dhe->bshe", normed, w_v, preferred_element_type=jnp.float32).astype(jnp.bfloat16)
    q_grouped = queries.reshape(batch, seq_len, kv_heads, group, head_dim)
    scores = jnp.einsum("bqkgd,bskd->bkgqs", q_grouped, keys_rot, preferred_element_type=jnp.float32) * head_dim ** -0.5
    row_pos = lax.broadcasted_iota(jnp.int32, (seq_len, seq_len), 0)
    col_pos = lax.broadcasted_iota(jnp.int32, (seq_len, seq_len), 1)
    probs = jax.nn.softmax(jnp.where(row_pos >= col_pos, scores, -jnp.inf), axis=-1).astype(jnp.bfloat16)
    attended = jnp.einsum("bkgqs,bskd->bqkgd", probs, values, preferred_element_type=jnp.float32).astype(jnp.bfloat16)
    attended = attended.reshape(batch, seq_len, heads * head_dim)
    after_attn = (hidden.astype(jnp.float32) + jnp.einsum("bsf,fd->bsd", attended, w_o, preferred_element_type=jnp.float32)).astype(jnp.bfloat16)
    mlp_in = rms_norm(after_attn, mlp_gain)
    gate_proj = jnp.einsum("bsd,df->bsf", mlp_in, w_gate, preferred_element_type=jnp.float32).astype(jnp.bfloat16)
    up_proj = jnp.einsum("bsd,df->bsf", mlp_in, w_up, preferred_element_type=jnp.float32).astype(jnp.bfloat16)
    gated = (jax.nn.silu(gate_proj.astype(jnp.float32)) * up_proj.astype(jnp.float32)).astype(jnp.bfloat16)
    return (after_attn.astype(jnp.float32) + jnp.einsum("bsf,fd->bsd", gated, w_down, preferred_element_type=jnp.float32)).astype(jnp.bfloat16)


def solution(mesh):
    batch_spec = P(("dp", "fsdp"), None, None)
    gain_spec = P(None, "fsdp")
    proj_spec = P(None, "fsdp", None, None)
    mat_spec = P(None, "fsdp", None)

    def local_forward(hidden, attn_norm, w_q, w_k, w_v, w_o, mlp_norm, w_gate, w_up, w_down):
        for layer in range(w_q.shape[0]):
            whole = [lax.all_gather(shard[layer], "fsdp", axis=0, tiled=True) for shard in (attn_norm, w_q, w_k, w_v, w_o, mlp_norm, w_gate, w_up, w_down)]
            hidden = decoder_layer(hidden, whole[0], whole[1], whole[2], whole[3], whole[4], whole[5], whole[6], whole[7], whole[8])
        return hidden

    return jax.shard_map(local_forward, mesh=mesh, in_specs=(batch_spec, gain_spec, proj_spec, proj_spec, proj_spec, mat_spec, gain_spec, mat_spec, mat_spec, mat_spec), out_specs=batch_spec, check_vma=False)
```

profile of v0, /device:TPU:0, one launch (start us, length us, event | category | flops | bytes accessed | tf_op | source)
XLA Modules:
  0.0 1979.0 jit_solution(2192846933224587295)
XLA Ops:
  6.5 1.5 fusion.215
  8.0 1.4 copy.50
  9.5 4.6 fusion.214
  14.0 4.5 copy.51
  18.6 2.6 slice_bitcast_fusion
  21.3 4.8 fusion.213
  26.2 10.4 fusion.210
  36.7 10.4 fusion.211
  47.1 10.6 fusion.212
  57.9 2.9 copy.54
  60.8 1.4 copy.53
  62.3 0.5 all-gather.47.cloned.1.call-update
  62.9 0.7 all-gather.53.cloned.1.call-update
  64.2 0.7 all-gather.57.cloned.1.call-update
  65.7 13.7 all-gather
  79.4 10.9 all-gather.5
  90.3 10.9 all-gather.9
  101.3 10.9 all-gather.14
  112.7 4.6 fusion.174
  117.5 34.9 %all-gather.37.cloned.1.call-done = bf16[1,3072,24,128]{1,3,2,0:T(8,128)(2,1)} async-done(((bf16[1,384,24,128]{1,3,2,0:T(8,128)(2,1)}), bf16[1,3072,24,128]{1,3,2,0:T(8,128)(2,1)}) %all-gather.37.cloned.1.call-update) | async-done | bytes 18874384 | tf_op jit(solution)/shard_map/all_gather | solution.py:64
  152.4 9.3 fusion.176
  162.4 1.2 copy.27
  163.5 1.9 fusion.218
  165.7 28.0 %all-gather.33.cloned.1.call-done = bf16[1,3072,8,128]{3,2,0,1:T(8,128)(2,1)} async-done(((bf16[1,384,8,128]{3,2,0,1:T(8,128)(2,1)}), bf16[1,3072,8,128]{3,2,0,1:T(8,128)(2,1)}) %all-gather.33.cloned.1.call-update) | async-done | bytes 6291472 | tf_op jit(solution)/shard_map/all_gather | solution.py:64
  193.8 5.6 convolution_convert_fusion.1
  199.4 89.0 %all-gather.39.cloned.1.call-done = bf16[1,3072,3072]{2,1,0:T(8,128)(2,1)} async-done(((bf16[1,384,3072]{2,1,0:T(8,128)(2,1)}), bf16[1,3072,3072]{2,1,0:T(8,128)(2,1)}) %all-gather.39.cloned.1.call-update) | async-done | bytes 18874384 | tf_op jit(solution)/shard_map/all_gather | solution.py:64
  288.4 7.9 multiply_reduce_fusion.2
  296.4 220.4 %all-gather.41.cloned.1.call-done = bf16[1,3072,8192]{2,1,0:T(8,128)(2,1)} async-done(((bf16[1,384,8192]{2,1,0:T(8,128)(2,1)}), bf16[1,3072,8192]{2,1,0:T(8,128)(2,1)}) %all-gather.41.cloned.1.call-update) | async-done | bytes 50331664 | tf_op jit(solution)/shard_map/all_gather | solution.py:64
  516.8 20.9 %fusion.19 = f32[128,8192]{1,0:T(8,128)} fusion(bf16[1,3072,8192]{2,1,0:T(8,128)(2,1)} %all-gather.41.cloned.1.call-done, f32[1,128,3072]{2,1,0:T(8,128)S(1)} %get-tuple-element.36, f32[3072]{0:T(1024)S(1)} %bitcast.285, f32[128]{0:T(128)S(1)} %add_rsqrt_fusion.2), kind=kOutput, calls=%fused_computation.17 | convolution fusion | flops 6445727744 | bytes 56111616 | tf_op jit(solution)/shard_map/bsd,df->bsf/dot_general | solution.py:50
  537.6 207.5 %all-gather.43.cloned.1.call-done = bf16[1,3072,8192]{2,1,0:T(8,128)(2,1)} async-done(((bf16[1,384,8192]{2,1,0:T(8,128)(2,1)}), bf16[1,3072,8192]{2,1,0:T(8,128)(2,1)}) %all-gather.43.cloned.1.call-update) | async-done | bytes 50331664 | tf_op jit(solution)/shard_map/all_gather | solution.py:64
  745.1 228.5 %all-gather.45.cloned.1.call-done = bf16[1,8192,3072]{2,1,0:T(8,128)(2,1)} async-done(((bf16[1,1024,3072]{2,1,0:T(8,128)(2,1)}), bf16[1,8192,3072]{2,1,0:T(8,128)(2,1)}) %all-gather.45.cloned.1.call-update) | async-done | bytes 50331664 | tf_op jit(solution)/shard_map/all_gather | solution.py:64
  973.6 37.0 %multiply_reduce_fusion.1 = (f32[128]{0:T(128)S(1)}, f32[1,128,3072]{2,1,0:T(8,128)}) fusion(f32[1,128,3072]{2,1,0:T(8,128)S(1)} %get-tuple-element.36, bf16[1,8192,3072]{2,1,0:T(8,128)(2,1)} %all-gather.45.cloned.1.call-done, bf16[1,3072,8192]{2,1,0:T(8,128)(2,1)} %all-gather.43.cloned.1.call-done, f32[128,8192]{1,0:T(8,128)} %fusion.19, ...), kind=kOutput, calls=%fused_computation.69 | convolution fusion | flops 12896436224 | bytes 108016640 | tf_op jit(solution)/shard_map/bsf,fd->bsd/dot_general | solution.py:53
  1010.6 1.6 multiply_convert_fusion.1
  1012.2 59.9 %all-gather.51.cloned.1.call-done = bf16[1,3072,24,128]{1,3,2,0:T(8,128)(2,1)} async-done(((bf16[1,384,24,128]{1,3,2,0:T(8,128)(2,1)}), bf16[1,3072,24,128]{1,3,2,0:T(8,128)(2,1)}) %all-gather.51.cloned.1.call-update) | async-done | bytes 18874384 | tf_op jit(solution)/shard_map/all_gather | solution.py:64
  1072.1 9.0 fusion.169
  1082.2 32.5 %all-gather.49.cloned.1.call-done = bf16[1,3072,8,128]{1,3,2,0:T(8,128)(2,1)} async-done(((bf16[1,384,8,128]{1,3,2,0:T(8,128)(2,1)}), bf16[1,3072,8,128]{1,3,2,0:T(8,128)(2,1)}) %all-gather.49.cloned.1.call-update) | async-done | bytes 6291472 | tf_op jit(solution)/shard_map/all_gather | solution.py:64
  1114.7 4.6 fusion.167
  1119.3 0.8 fusion.223
  1120.1 1.2 copy-done.2
  1121.6 34.3 %all-gather.47.cloned.1.call-done = bf16[1,3072,8,128]{3,2,0,1:T(8,128)(2,1)} async-done(((bf16[1,384,8,128]{3,2,0,1:T(8,128)(2,1)}), bf16[1,3072,8,128]{3,2,0,1:T(8,128)(2,1)}) %all-gather.47.cloned.1.call-update) | async-done | bytes 6291472 | tf_op jit(solution)/shard_map/all_gather | solution.py:64
  1155.9 7.0 convolution_convert_fusion
  1162.9 87.8 %all-gather.53.cloned.1.call-done = bf16[1,3072,3072]{2,1,0:T(8,128)(2,1)} async-done(((bf16[1,384,3072]{2,1,0:T(8,128)(2,1)}), bf16[1,3072,3072]{2,1,0:T(8,128)(2,1)}) %all-gather.53.cloned.1.call-update) | async-done | bytes 18874384 | tf_op jit(solution)/shard_map/all_gather | solution.py:64
  1250.7 8.1 multiply_reduce_fusion
  1258.9 220.2 %all-gather.55.cloned.1.call-done = bf16[1,3072,8192]{2,1,0:T(8,128)(2,1)} async-done(((bf16[1,384,8192]{2,1,0:T(8,128)(2,1)}), bf16[1,3072,8192]{2,1,0:T(8,128)(2,1)}) %all-gather.55.cloned.1.call-update) | async-done | bytes 50331664 | tf_op jit(solution)/shard_map/all_gather | solution.py:64
  1479.1 20.8 %fusion.37 = f32[128,8192]{1,0:T(8,128)} fusion(bf16[1,3072,8192]{2,1,0:T(8,128)(2,1)} %all-gather.55.cloned.1.call-done, f32[1,128,3072]{2,1,0:T(8,128)S(1)} %get-tuple-element.42, f32[3072]{0:T(1024)S(1)} %bitcast.283, f32[128]{0:T(128)S(1)} %add_rsqrt_fusion), kind=kOutput, calls=%fused_computation.23 | convolution fusion | flops 6445727744 | bytes 56111616 | tf_op jit(solution)/shard_map/bsd,df->bsf/dot_general | solution.py:50
  1499.9 207.6 %all-gather.57.cloned.1.call-done = bf16[1,3072,8192]{2,1,0:T(8,128)(2,1)} async-done(((bf16[1,384,8192]{2,1,0:T(8,128)(2,1)}), bf16[1,3072,8192]{2,1,0:T(8,128)(2,1)}) %all-gather.57.cloned.1.call-update) | async-done | bytes 50331664 | tf_op jit(solution)/shard_map/all_gather | solution.py:64
  1707.6 228.3 %all-gather.59.cloned.1.call-done = bf16[1,8192,3072]{2,1,0:T(8,128)(2,1)} async-done(((bf16[1,1024,3072]{2,1,0:T(8,128)(2,1)}), bf16[1,8192,3072]{2,1,0:T(8,128)(2,1)}) %all-gather.59.cloned.1.call-update) | async-done | bytes 50331664 | tf_op jit(solution)/shard_map/all_gather | solution.py:64
  1935.9 36.1 %fusion.122 = bf16[1,128,3072]{2,1,0:T(8,128)(2,1)} fusion(f32[1,128,3072]{2,1,0:T(8,128)S(1)} %get-tuple-element.42, bf16[1,8192,3072]{2,1,0:T(8,128)(2,1)} %all-gather.59.cloned.1.call-done, bf16[1,3072,8192]{2,1,0:T(8,128)(2,1)} %all-gather.57.cloned.1.call-done, f32[128,8192]{1,0:T(8,128)} %fusion.37, f32[3072]{0:T(1024)S(1)} %bitcast.284, ...), kind=kOutput, calls=%fused_computation.54 | convolution fusion | flops 12895256576 | bytes 107229696 | tf_op jit(solution)/shard_map/bsf,fd->bsd/dot_general | solution.py:53
  (60 shorter events, 4.8 us)
Async XLA Ops:
  6.5 106.2 %all-gather.35.cloned.1.call-start = ((), (), s32[]{:S(2)}) async-start(), calls=%async_computation.1 | async-start | bytes 7077888 | tf_op jit(solution)/shard_map/all_gather | solution.py:64
  9.4 143.0 %all-gather.37.cloned.1.call-start = ((), (), s32[]{:S(2)}) async-start(), calls=%async_computation.2 | async-start | bytes 21233664 | tf_op jit(solution)/shard_map/all_gather | solution.py:64
  18.5 175.2 %all-gather.33.cloned.1.call-start = ((), (), s32[]{:S(2)}) async-start(), calls=%async_computation | async-start | bytes 7077888 | tf_op jit(solution)/shard_map/all_gather | solution.py:64
  21.3 267.2 %all-gather.39.cloned.1.call-start = ((), (), s32[]{:S(2)}) async-start(), calls=%async_computation.3 | async-start | bytes 21233664 | tf_op jit(solution)/shard_map/all_gather | solution.py:64
  26.2 490.6 %all-gather.41.cloned.1.call-start = ((), (), s32[]{:S(2)}) async-start(), calls=%async_computation.4 | async-start | bytes 56623104 | tf_op jit(solution)/shard_map/all_gather | solution.py:64
  36.6 708.5 %all-gather.43.cloned.1.call-start = ((), (), s32[]{:S(2)}) async-start(), calls=%async_computation.5 | async-start | bytes 56623104 | tf_op jit(solution)/shard_map/all_gather | solution.py:64
  47.1 926.5 %all-gather.45.cloned.1.call-start = ((), (), s32[]{:S(2)}) async-start(), calls=%async_computation.6 | async-start | bytes 56623104 | tf_op jit(solution)/shard_map/all_gather | solution.py:64
  57.8 1014.3 %all-gather.51.cloned.1.call-start = ((), (), s32[]{:S(2)}) async-start(), calls=%async_computation.9 | async-start | bytes 21233664 | tf_op jit(solution)/shard_map/all_gather | solution.py:64
  60.8 1053.9 %all-gather.49.cloned.1.call-start = ((), (), s32[]{:S(2)}) async-start(), calls=%async_computation.8 | async-start | bytes 7077888 | tf_op jit(solution)/shard_map/all_gather | solution.py:64
  62.3 1093.6 %all-gather.47.cloned.1.call-start = ((), (), s32[]{:S(2)}) async-start(), calls=%async_computation.7 | async-start | bytes 7077888 | tf_op jit(solution)/shard_map/all_gather | solution.py:64
  62.9 1187.9 %all-gather.53.cloned.1.call-start = ((), (), s32[]{:S(2)}) async-start(), calls=%async_computation.10 | async-start | bytes 21233664 | tf_op jit(solution)/shard_map/all_gather | solution.py:64
  63.6 1415.5 %all-gather.55.cloned.1.call-start = ((), (), s32[]{:S(2)}) async-start(), calls=%async_computation.11 | async-start | bytes 56623104 | tf_op jit(solution)/shard_map/all_gather | solution.py:64
  64.2 1643.4 %all-gather.57.cloned.1.call-start = ((), (), s32[]{:S(2)}) async-start(), calls=%async_computation.12 | async-start | bytes 56623104 | tf_op jit(solution)/shard_map/all_gather | solution.py:64
  64.9 1871.0 %all-gather.59.cloned.1.call-start = ((), (), s32[]{:S(2)}) async-start(), calls=%async_computation.13 | async-start | bytes 56623104 | tf_op jit(solution)/shard_map/all_gather | solution.py:64
  65.0 0.7 copy-start.3
  65.0 14.4 copy-start.4
  65.0 47.2 %copy-start = (bf16[1,128,3072]{2,1,0:T(8,128)(2,1)S(1)}, bf16[1,128,3072]{2,1,0:T(8,128)(2,1)}, u32[]{:S(2)}) copy-start(bf16[1,128,3072]{2,1,0:T(8,128)(2,1)} %param.10) | copy-start | bytes 2359300
  112.5 39.9 %copy-start.5 = (f32[128]{0:T(128)}, f32[128]{0:T(128)S(1)}, u32[]{:S(2)}) copy-start(f32[128]{0:T(128)S(1)} %add_rsqrt_fusion.3) | copy-start | bytes 1540
  1120.1 1.2 copy-start.2
  1155.9 94.8 %copy-start.1 = (f32[1,128,3072]{2,1,0:T(8,128)S(1)}, f32[1,128,3072]{2,1,0:T(8,128)}, u32[]{:S(2)}) copy-start(f32[1,128,3072]{2,1,0:T(8,128)} %get-tuple-element.38) | copy-start | bytes 4718596
Sparse Core Ops, SparseCore 0:
  9.5 43.5 all-gather.34
  54.9 97.3 all-gather.36
  154.2 39.5 all-gather.32
  195.4 92.9 all-gather.38
  290.1 226.6 all-gather.40
  518.5 226.6 all-gather.42
  746.9 226.5 all-gather.44
  975.4 96.6 all-gather.50
  1073.9 40.7 all-gather.48
  1116.3 39.5 all-gather.46
  1157.7 92.9 all-gather.52
  1252.4 226.6 all-gather.54
  1480.9 226.5 all-gather.56
  1709.2 226.6 all-gather.58
where the time goes:
time: 1990 us; the launch traced here: 1980 us
  waiting for transfers between devices  1680 us (84%)
  matrix products  174 us (9%)
  local copies, waits for them, and re-layouts  58.8 us (3%)
  blocking collectives  46.4 us (2%)
    all_gather x14, waiting for transfers between devices, local_forward(): lax.all_gather(shard[layer], 'fsdp', axis=0, tiled=True)  1680 us
    dot_general x2, matrix products, decoder_layer(): jnp.einsum('bsf,fd->bsd', gated, w_down, preferred_element_type=jnp.float32)  73.1 us
    all_gather x4, blocking collectives, local_forward(): lax.all_gather(shard[layer], 'fsdp', axis=0, tiled=True)  46.4 us
    slice x8, local copies, waits for them, and re-layouts, local_forward(): shard[layer]  42.3 us
    dot_general x2, matrix products, decoder_layer(): jnp.einsum('bsd,df->bsf', mlp_in, w_gate, preferred_element_type=jnp.floa...  41.7 us
  transfers between devices with their start and end apart: 14, of which 13 were waited for; matrix products, arithmetic and copies ran while one was open for 10% of the time, Pallas kernels for 0%

commit v1 on v0

v1 whole, which is shorter than its diff:
```python
import functools

import jax
import jax.numpy as jnp
import numpy as np
from jax import lax
from jax.experimental import pallas as pl
from jax.experimental.pallas import tpu as pltpu
from jax.sharding import PartitionSpec as P

ROPE_THETA = 500000.0
NORM_EPS = 1e-5
MESH = pl.DeviceIdType.MESH
F32 = jnp.float32
BF16 = jnp.bfloat16

DEV = 8
CHIPS = 4
SEQ = 128
DIM = 3072
HALF = DIM // 2
ROWS = DIM // DEV
HD = 128
QH = 3
QCOLS = QH * HD
QKV = QCOLS + 2 * HD
FFN = 8192
FCOLS = FFN // DEV
NCH = 4
CW = FCOLS // NCH
LAYERS = 2


def rope_tables():
    half = HD // 2
    inv_freq = np.power(np.float32(ROPE_THETA), -(np.arange(half, dtype=np.float32) * np.float32(2.0) / np.float32(HD)))
    angles = (np.arange(SEQ, dtype=np.float32)[:, None] * inv_freq.astype(np.float32)[None, :]).astype(np.float64)
    cos, sin = np.cos(angles).astype(np.float32), np.sin(angles).astype(np.float32)
    return np.concatenate([cos, cos], axis=1), np.concatenate([-sin, sin], axis=1)


def body(x_in, g_in, cos_in, sin_in, wqkv_in, wo_in, wg_in, wu_in, wd_in,
         out, land_qkv, land_gu,
         xb, u, part, rm, r1, r2, wqkv, wo, wd, wgu, qb, kb, vb, ob, zb, gains,
         ss_qkv, rs_qkv, ss_gu, rs_gu, s_gain, l_sem, ld_sem,
         ag_s, ag_r, mt_s, mt_r, r1_s, r1_r, r2_s, r2_r):
    me = lax.axis_index("fsdp")
    c = me % 2
    cx = (me // 2) % 2
    cy = me // 4
    chip = me // 2

    def dev(fy, fx, fc):
        yy = 1 - cy if fy else cy
        xx = 1 - cx if fx else cx
        cc = 1 - c if fc else c
        return yy * 4 + xx * 2 + cc

    mate, xn, yn = dev(0, 0, 1), dev(0, 1, 0), dev(1, 0, 0)
    chip_x, chip_y, chip_d = xn // 2, yn // 2, dev(1, 1, 0) // 2
    flips = ((1, 1, 0), (1, 1, 1), (0, 1, 0), (1, 0, 0), (0, 1, 1), (1, 0, 1), (0, 0, 1))

    def remote(src, dst, ssem, rsem, target):
        return pltpu.make_async_remote_copy(src, dst, ssem, rsem, device_id={"fsdp": target}, device_id_type=MESH)

    def bytes_wait(ref, sem):
        pltpu.make_async_copy(ref, ref, sem).wait()

    barrier = pltpu.get_barrier_semaphore()
    for f in flips:
        pl.semaphore_signal(barrier, inc=1, device_id={"fsdp": dev(*f)}, device_id_type=MESH)
    pl.semaphore_wait(barrier, DEV - 1)

    def send_qkv(l):
        for f in flips:
            e = dev(*f)
            remote(wqkv_in.at[l, :, pl.ds(pl.multiple_of(e * QKV, 128), QKV)],
                   land_qkv.at[l, pl.ds(pl.multiple_of(me * ROWS, ROWS), ROWS), :],
                   ss_qkv.at[l], rs_qkv.at[l], e).start()

    def send_gu(l, n):
        for f in flips:
            e = dev(*f)
            cols = pl.ds(pl.multiple_of(e * FCOLS + n * CW, 128), CW)
            rows = pl.ds(pl.multiple_of(me * ROWS, ROWS), ROWS)
            remote(wg_in.at[l, :, cols], land_gu.at[l, n, rows, pl.ds(0, CW)], ss_gu.at[l, n], rs_gu.at[l, n], e).start()
            remote(wu_in.at[l, :, cols], land_gu.at[l, n, rows, pl.ds(CW, CW)], ss_gu.at[l, n], rs_gu.at[l, n], e).start()

    OTHER = (DEV - 1) * ROWS

    def load_qkv(l):
        for f in flips:
            rows = pl.ds(pl.multiple_of(dev(*f) * ROWS, ROWS), ROWS)
            pltpu.make_async_copy(land_qkv.at[l, rows, :], wqkv.at[rows, :], ld_sem.at[0]).start()
        mine = pl.ds(pl.multiple_of(me * ROWS, ROWS), ROWS)
        pltpu.make_async_copy(wqkv_in.at[l, :, pl.ds(pl.multiple_of(me * QKV, 128), QKV)], wqkv.at[mine, :], ld_sem.at[0]).start()

    def load_gu(l, n):
        slot = n % 2
        for f in flips:
            rows = pl.ds(pl.multiple_of(dev(*f) * ROWS, ROWS), ROWS)
            pltpu.make_async_copy(land_gu.at[l, n, rows, :], wgu.at[slot, rows, :], ld_sem.at[1 + slot]).start()
        mine = pl.ds(pl.multiple_of(me * ROWS, ROWS), ROWS)
        cols = pl.ds(pl.multiple_of(me * FCOLS + n * CW, 128), CW)
        pltpu.make_async_copy(wg_in.at[l, :, cols], wgu.at[slot, mine, pl.ds(0, CW)], ld_sem.at[1 + slot]).start()
        pltpu.make_async_copy(wu_in.at[l, :, cols], wgu.at[slot, mine, pl.ds(CW, CW)], ld_sem.at[1 + slot]).start()

    my_slot = c * CHIPS + chip

    def norm(row):
        def one(i, carry):
            rows = pl.ds(pl.multiple_of(i * 16, 16), 16)
            wide = xb[rows, :].astype(F32)
            inv = lax.rsqrt(jnp.mean(wide * wide, axis=-1, keepdims=True) + NORM_EPS)
            for s in range(DEV):
                cols = slice(s * ROWS, (s + 1) * ROWS)
                g = gains[s, pl.ds(row, 1), :]
                u[my_slot, rows, cols] = (wide[:, cols] * inv * g).astype(BF16)
            return carry
        lax.fori_loop(0, SEQ // 16, one, 0)

    A, B = pl.ds(0, HALF), pl.ds(HALF, HALF)

    def u_copy(slot, cols, k, target):
        ref = u.at[slot, :, cols] if cols is not None else u.at[slot]
        return remote(ref, ref, ag_s.at[k], ag_r.at[k], target)

    def gather_start():
        u_copy(my_slot, A, 0, xn).start()
        u_copy(my_slot, B, 1, yn).start()
        u_copy(my_slot, B, 2, xn).start()
        u_copy(my_slot, A, 3, yn).start()
        u_copy(my_slot, None, 6, mate).start()

    def gather_forward():
        base = c * CHIPS
        u_copy(base + chip_x, A, 0, xn).wait_recv()
        u_copy(base + chip_x, A, 4, yn).start()
        u_copy(base + chip_y, B, 1, yn).wait_recv()
        u_copy(base + chip_y, B, 5, xn).start()

    def gather_finish():
        base = c * CHIPS
        u_copy(base + chip_x, B, 2, xn).wait_recv()
        u_copy(base + chip_x, None, 7, mate).start()
        u_copy(base + chip_y, A, 3, yn).wait_recv()
        u_copy(base + chip_y, None, 8, mate).start()
        u_copy(base + chip_d, A, 4, yn).wait_recv()
        u_copy(base + chip_d, B, 5, xn).wait_recv()
        u_copy(base + chip_d, None, 9, mate).start()
        for k in (6, 7, 8, 9):
            u_copy(my_slot, None, k, mate).wait_recv()
        for k in range(6):
            u_copy(my_slot, A, k, xn).wait_send()
        for k in (6, 7, 8, 9):
            u_copy(my_slot, None, k, mate).wait_send()

    def reduce_scatter(lhs, rhs, after_stage1, after_stage2):
        own, other = c * CHIPS, (1 - c) * CHIPS
        order = ((chip_d, chip_x, chip_y, chip), (chip_d, chip_y, chip_x, chip))
        first = (xn, yn)
        second = (yn, xn)
        TN = 512

        def hcols(h):
            return pl.ds(h * HALF, HALF)

        def mate_copy(h, k):
            return remote(part.at[other + order[h][k], :, hcols(h)], rm.at[order[h][k], :, hcols(h)],
                          mt_s.at[h, k], mt_r.at[h, k], mate)

        def stage1(h, k):
            return remote(part.at[own + order[h][k], :, hcols(h)], r1.at[h, k], r1_s.at[h, k], r1_r.at[h, k], first[h])

        def stage2(h):
            return remote(part.at[own + order[h][2], :, hcols(h)], r2.at[h], r2_s.at[h], r2_r.at[h], second[h])

        def fold(h, k, extra):
            j = order[h][k]

            def one(i, carry):
                rows = pl.ds(pl.multiple_of(i * 8, 8), 8)
                total = part[own + j, rows, hcols(h)] + rm[j, rows, hcols(h)]
                if extra is not None:
                    total = total + extra[rows, :]
                part[own + j, rows, hcols(h)] = total
                return carry
            lax.fori_loop(0, SEQ // 8, one, 0)

        for h in range(2):
            for grp in (other, own):
                a = lhs(grp)

                def tile(t, carry, grp=grp, h=h, a=a):
                    cols = pl.ds(pl.multiple_of(h * HALF + t * TN, TN), TN)
                    prod = jnp.dot(a, rhs[:, cols], preferred_element_type=F32)
                    part[pl.ds(grp, CHIPS), :, cols] = prod.reshape(CHIPS, SEQ, TN)
                    return carry
                lax.fori_loop(0, HALF // TN, tile, 0)
                if grp is other:
                    for k in range(4):
                        mate_copy(h, k).start()
            for k in (0, 1):
                mate_copy(h, k).wait_recv()
                fold(h, k, None)
                stage1(h, k).start()
        after_stage1()
        for h in range(2):
            mate_copy(h, 2).wait_recv()
            stage1(h, 0).wait_recv()
            fold(h, 2, r1.at[h, 0])
            stage2(h).start()
        after_stage2()
        for h in range(2):
            mate_copy(h, 3).wait_recv()
            stage1(h, 1).wait_recv()
            stage2(h).wait_recv()

            def last(i, carry, h=h):
                rows = pl.ds(pl.multiple_of(i * 16, 16), 16)
                total = (part[own + chip, rows, hcols(h)] + rm[chip, rows, hcols(h)]) + (r1[h, 1, rows, :] + r2[h, rows, :])
                xb[rows, hcols(h)] = (xb[rows, hcols(h)].astype(F32) + total).astype(BF16)
                return carry
            lax.fori_loop(0, SEQ // 16, last, 0)
        for h in range(2):
            for k in range(4):
                mate_copy(h, k).wait_send()
            for k in range(2):
                stage1(h, k).wait_send()
            stage2(h).wait_send()

    def nothing():
        pass

    own_x = pltpu.make_async_copy(x_in, xb, l_sem.at[2])
    own_x.start()
    for f in flips:
        remote(g_in, gains.at[me], s_gain.at[0], s_gain.at[1], dev(*f)).start()
    own_g = pltpu.make_async_copy(g_in, gains.at[me], l_sem.at[3])
    own_g.start()
    send_qkv(0)
    own_x.wait()
    own_g.wait()
    bytes_wait(gains.at[pl.ds(0, DEV - 1)], s_gain.at[1])
    bytes_wait(gains.at[pl.ds(0, DEV - 1)], s_gain.at[0])

    def layer(l, carry):
        ld_o = pltpu.make_async_copy(wo_in.at[l], wo, l_sem.at[0])
        ld_d = pltpu.make_async_copy(wd_in.at[l], wd, l_sem.at[1])
        ld_o.start()
        ld_d.start()
        norm(2 * l)
        gather_start()
        gather_forward()
        send_gu(l, 0)
        bytes_wait(land_qkv.at[l, pl.ds(0, OTHER), :], rs_qkv.at[l])
        load_qkv(l)
        gather_finish()
        bytes_wait(wqkv, ld_sem.at[0])

        def qkv_block(i, carry):
            prod = jnp.dot(u[pl.ds(i * 2, 2)].reshape(2 * SEQ, DIM), wqkv[...], preferred_element_type=F32)
            cos, sin = cos_in[...], sin_in[...]
            for s in range(2):
                rows = slice(s * SEQ, (s + 1) * SEQ)
                for h in range(QH + 1):
                    head = prod[rows, h * HD:(h + 1) * HD]
                    rot = (head * cos + pltpu.roll(head, HD // 2, 1) * sin).astype(BF16)
                    if h < QH:
                        qb[i * 2 + s, pl.ds(h * SEQ, SEQ), :] = rot
                    else:
                        kb[i * 2 + s] = rot
                vb[i * 2 + s] = prod[rows, (QH + 1) * HD:].astype(BF16)
            return carry
        lax.fori_loop(0, DEV // 2, qkv_block, 0)

        def attend(s, carry):
            scores = lax.dot_general(qb[s], kb[s], (((1,), (1,)), ((), ())), preferred_element_type=F32) * HD ** -0.5
            row = lax.broadcasted_iota(jnp.int32, (QH * SEQ, SEQ), 0) % SEQ
            col = lax.broadcasted_iota(jnp.int32, (QH * SEQ, SEQ), 1)
            scores = jnp.where(row >= col, scores, -jnp.inf)
            e = jnp.exp(scores - jnp.max(scores, axis=-1, keepdims=True))
            probs = (e / jnp.sum(e, axis=-1, keepdims=True)).astype(BF16)
            o = jnp.dot(probs, vb[s], preferred_element_type=F32).astype(BF16)
            for h in range(QH):
                ob[s, :, h * HD:(h + 1) * HD] = o[h * SEQ:(h + 1) * SEQ]
            return carry
        lax.fori_loop(0, DEV, attend, 0)

        ld_o.wait()
        reduce_scatter(lambda grp: ob[pl.ds(grp, CHIPS)].reshape(CHIPS * SEQ, QCOLS), wo,
                       lambda: send_gu(l, 1), lambda: send_gu(l, 2))

        norm(2 * l + 1)
        gather_start()
        gather_forward()
        send_gu(l, 3)
        for n in range(2):
            bytes_wait(land_gu.at[l, n, pl.ds(0, OTHER), :], rs_gu.at[l, n])
            load_gu(l, n)
        gather_finish()

        @pl.when(l + 1 < LAYERS)
        def _():
            send_qkv(l + 1)

        for n in range(NCH):
            slot = n % 2
            bytes_wait(wgu.at[slot], ld_sem.at[1 + slot])

            def mlp_block(i, carry, n=n, slot=slot):
                prod = jnp.dot(u[pl.ds(i * 4, 4)].reshape(4 * SEQ, DIM), wgu[slot], preferred_element_type=F32)
                gate = prod[:, :CW].astype(BF16).astype(F32)
                up = prod[:, CW:].astype(BF16).astype(F32)
                z = (gate * jax.nn.sigmoid(gate) * up).astype(BF16)
                zb[pl.ds(i * 4, 4), :, n * CW:(n + 1) * CW] = z.reshape(4, SEQ, CW)
                return carry
            lax.fori_loop(0, 2, mlp_block, 0)
            if n + 2 < NCH:
                bytes_wait(land_gu.at[l, n + 2, pl.ds(0, OTHER), :], rs_gu.at[l, n + 2])
                load_gu(l, n + 2)

        ld_d.wait()
        reduce_scatter(lambda grp: zb[pl.ds(grp, CHIPS)].reshape(CHIPS * SEQ, FCOLS), wd, nothing, nothing)

        bytes_wait(land_qkv.at[l, pl.ds(0, OTHER), :], ss_qkv.at[l])
        for n in range(NCH):
            bytes_wait(land_gu.at[l, n, pl.ds(0, OTHER), :], ss_gu.at[l, n])
        return carry

    lax.fori_loop(0, LAYERS, layer, 0)
    done = pltpu.make_async_copy(xb, out, l_sem.at[2])
    done.start()
    done.wait()


def solution(mesh):
    batch_spec = P(("dp", "fsdp"), None, None)
    gain_spec = P(None, "fsdp")
    proj_spec = P(None, "fsdp", None, None)
    mat_spec = P(None, "fsdp", None)
    cos, sin = rope_tables()

    def local_forward(hidden, attn_norm, w_q, w_k, w_v, w_o, mlp_norm, w_gate, w_up, w_down):
        gains = jnp.stack([attn_norm[0], mlp_norm[0], attn_norm[1], mlp_norm[1]]).astype(F32)
        gains = jnp.pad(gains, ((0, 4), (0, 0)))
        wqkv = jnp.concatenate([w_q.reshape(LAYERS, ROWS, DEV, QCOLS), w_k.reshape(LAYERS, ROWS, DEV, HD),
                                w_v.reshape(LAYERS, ROWS, DEV, HD)], axis=-1).reshape(LAYERS, ROWS, DEV * QKV)
        hbm = pl.BlockSpec(memory_space=pltpu.HBM)
        vmem = pl.BlockSpec(memory_space=pltpu.VMEM)
        dma = pltpu.SemaphoreType.DMA
        out = pl.pallas_call(
            body,
            name="two_layers",
            out_shape=(jax.ShapeDtypeStruct((SEQ, DIM), BF16),
                       jax.ShapeDtypeStruct((LAYERS, DIM, QKV), BF16),
                       jax.ShapeDtypeStruct((LAYERS, NCH, DIM, 2 * CW), BF16)),
            in_specs=[hbm, vmem, vmem, vmem, hbm, hbm, hbm, hbm, hbm],
            out_specs=(hbm, hbm, hbm),
            scratch_shapes=[
                pltpu.VMEM((SEQ, DIM), BF16),
                pltpu.VMEM((DEV, SEQ, DIM), BF16),
                pltpu.VMEM((DEV, SEQ, DIM), F32),
                pltpu.VMEM((CHIPS, SEQ, DIM), F32),
                pltpu.VMEM((2, 2, SEQ, HALF), F32),
                pltpu.VMEM((2, SEQ, HALF), F32),
                pltpu.VMEM((DIM, QKV), BF16),
                pltpu.VMEM((QCOLS, DIM), BF16),
                pltpu.VMEM((FCOLS, DIM), BF16),
                pltpu.VMEM((2, DIM, 2 * CW), BF16),
                pltpu.VMEM((DEV, QH * SEQ, HD), BF16),
                pltpu.VMEM((DEV, SEQ, HD), BF16),
                pltpu.VMEM((DEV, SEQ, HD), BF16),
                pltpu.VMEM((DEV, SEQ, QCOLS), BF16),
                pltpu.VMEM((DEV, SEQ, FCOLS), BF16),
                pltpu.VMEM((DEV, 8, ROWS), F32),
                dma((LAYERS,)), dma((LAYERS,)), dma((LAYERS, NCH)), dma((LAYERS, NCH)), dma((2,)), dma((4,)), dma((3,)),
                dma((10,)), dma((10,)), dma((2, 4)), dma((2, 4)), dma((2, 2)), dma((2, 2)), dma((2,)), dma((2,)),
            ],
            compiler_params=pltpu.CompilerParams(collective_id=0, has_side_effects=True, vmem_limit_bytes=66_000_000),
        )(hidden[0], gains, cos, sin, wqkv, w_o, w_gate, w_up, w_down)[0]
        return out[None]

    return jax.shard_map(local_forward, mesh=mesh, in_specs=(batch_spec, gain_spec, proj_spec, proj_spec, proj_spec, mat_spec, gain_spec, mat_spec, mat_spec, mat_spec), out_specs=batch_spec, check_vma=False)
```

time: 1990 us -> 732 us (0.37)
  waiting for transfers between devices: 1680 us -> 0 us
  Pallas kernels: 0 us -> 701 us
  matrix products: 174 us -> 0 us
  blocking collectives: 46.4 us -> 0 us
  local copies, waits for them, and re-layouts: 58.8 us -> 23.6 us
    all_gather x14 -> x0, waiting for transfers between devices: 1680 us -> none  [local_forward(): lax.all_gather(shard[layer], 'fsdp', axis=0, tiled=True)]
    pallas_call x0 -> x1, Pallas kernels: none -> 701 us  [local_forward(): pl.pallas_call(body, name='two_layers', out_shape=(jax.ShapeDtypeStruct((...]
    dot_general x10 -> x0, matrix products: 146 us -> none  [the longest x2 73.1 us: decoder_layer(): jnp.einsum('bsf,fd->bsd', gated, w_down, preferred_element_type=jnp.float32)]
    all_gather x4 -> x0, blocking collectives: 46.4 us -> none  [local_forward(): lax.all_gather(shard[layer], 'fsdp', axis=0, tiled=True)]
    slice x8 -> x1, local copies, waits for them, and re-layouts: 42.3 us -> 0.89 us  [local_forward(): attn_norm[0]]
    unnamed x4 -> x0, matrix products: 27.6 us -> none
    reshape x0 -> x2, local copies, waits for them, and re-layouts: none -> 20.7 us  [the longest x1 12.3 us: local_forward(): wqkv = jnp.concatenate([w_q.reshape(LAYERS, ROWS, DEV, QCOLS), w_k.reshap...]
  transfers between devices with their start and end apart: 14 -> 0, of which waited for: 13 -> 0; matrix products, arithmetic and copies ran while one was open for 10% -> 0% of each run, Pallas kernels for 0% -> 0%
where the time goes in v1:
time: 732 us; the launch traced here: 731 us
  Pallas kernels  701 us (96%)
  local copies, waits for them, and re-layouts  23.6 us (3%)
    pallas_call x1, Pallas kernels, local_forward(): pl.pallas_call(body, name='two_layers', out_shape=(jax.ShapeDtypeStruct((...  701 us

profile of v1, /device:TPU:0, one launch (start us, length us, event | category | flops | bytes accessed | tf_op | source)
XLA Modules:
  0.0 730.9 jit_solution(10795552242307583211)
XLA Ops:
  0.0 0.0 copy-start
  0.0 0.0 copy-start.1
  0.0 0.9 fusion.8
  0.9 0.6 fusion.7.g_in
  1.5 8.3 %reshape.6 = bf16[2,384,8,384]{3,2,1,0:T(8,128)(2,1)} reshape(bf16[2,384,24,128]{3,2,1,0:T(8,128)(2,1)} %param.14) | data formatting | bytes 9437184 | tf_op jit(solution)/shard_map/reshape | solution.py:347
  9.8 0.0 copy-done
  9.8 0.0 copy-done.1
  9.8 6.1 pad_maximum_fusion
  15.9 12.3 %reshape.7.wqkv_in = bf16[2,384,5120]{2,1,0:T(8,128)(2,1)} reshape(bf16[2,384,8,640]{3,2,1,0:T(8,128)(2,1)} %pad_maximum_fusion) | data formatting | bytes 15728640 | tf_op jit(solution)/shard_map/reshape | solution.py:348
  28.3 700.5 %two_layers.1 = (bf16[128,3072]{1,0:T(8,128)(2,1)}, bf16[2,3072,640]{2,1,0:T(8,128)(2,1)}, bf16[2,4,3072,512]{3,2,1,0:T(8,128)(2,1)}) custom-call(bf16[128,3072]{1,0:T(8,128)(2,1)} %bitcast.7, f32[8,384]{1,0:T(8,128)} %fusion.7.g_in, f32[128,128]{1,0:T(8,128)} %constant.8.clone.cos_in, f32[128,128]{1,0:T(8,128)} %constant.9.clone.sin_in, ...), custom_call_target="tpu_custom_call" | custom-call | tf_op jit(solution)/shard_map/two_layers/pallas_call | solution.py:352
  728.8 2.1 copy.14
Async XLA Ops:
  0.0 9.8 %copy-start = (bf16[2,384,8,128]{3,2,1,0:T(8,128)(2,1)S(1)}, bf16[2,384,8,128]{3,2,1,0:T(8,128)(2,1)}, u32[]{:S(2)}) copy-start(bf16[2,384,8,128]{3,2,1,0:T(8,128)(2,1)} %param.16) | copy-start | bytes 4718596
  0.0 9.8 %copy-start.1 = (bf16[2,384,8,128]{3,2,1,0:T(8,128)(2,1)S(1)}, bf16[2,384,8,128]{3,2,1,0:T(8,128)(2,1)}, u32[]{:S(2)}) copy-start(bf16[2,384,8,128]{3,2,1,0:T(8,128)(2,1)} %param.15) | copy-start | bytes 4718596

commit v2 on v1

--- a/solution.py
+++ b/solution.py
@@ -29,6 +29,9 @@
 NCH = 4
 CW = FCOLS // NCH
 LAYERS = 2
+RB = 96
+NP = 4
+PW = DIM // NP
 
 
 def rope_tables():
@@ -39,11 +42,11 @@
     return np.concatenate([cos, cos], axis=1), np.concatenate([-sin, sin], axis=1)
 
 
-def body(x_in, g_in, cos_in, sin_in, wqkv_in, wo_in, wg_in, wu_in, wd_in,
-         out, land_qkv, land_gu,
-         xb, u, part, rm, r1, r2, wqkv, wo, wd, wgu, qb, kb, vb, ob, zb, gains,
+def body(x_in, g_in, cos_in, sin_in, wq_in, wk_in, wv_in, wo_in, wg_in, wu_in, wd_in,
+         out, stage_qkv, land_qkv, land_gu,
+         rq, rk, rv, st, xb, u, part, rm, r1, r2, wqkv, wo, wd, wgu, qb, kb, vb, ob, zb, gains,
          ss_qkv, rs_qkv, ss_gu, rs_gu, s_gain, l_sem, ld_sem,
-         ag_s, ag_r, mt_s, mt_r, r1_s, r1_r, r2_s, r2_r):
+         rl_in, rl_out, ag_s, ag_r, mt_s, mt_r, r1_s, r1_r, r2_s, r2_r):
     me = lax.axis_index("fsdp")
     c = me % 2
     cx = (me // 2) % 2
@@ -74,7 +77,7 @@
     def send_qkv(l):
         for f in flips:
             e = dev(*f)
-            remote(wqkv_in.at[l, :, pl.ds(pl.multiple_of(e * QKV, 128), QKV)],
+            remote(stage_qkv.at[l, e],
                    land_qkv.at[l, pl.ds(pl.multiple_of(me * ROWS, ROWS), ROWS), :],
                    ss_qkv.at[l], rs_qkv.at[l], e).start()
 
@@ -93,7 +96,7 @@
             rows = pl.ds(pl.multiple_of(dev(*f) * ROWS, ROWS), ROWS)
             pltpu.make_async_copy(land_qkv.at[l, rows, :], wqkv.at[rows, :], ld_sem.at[0]).start()
         mine = pl.ds(pl.multiple_of(me * ROWS, ROWS), ROWS)
-        pltpu.make_async_copy(wqkv_in.at[l, :, pl.ds(pl.multiple_of(me * QKV, 128), QKV)], wqkv.at[mine, :], ld_sem.at[0]).start()
+        pltpu.make_async_copy(stage_qkv.at[l, me], wqkv.at[mine, :], ld_sem.at[0]).start()
 
     def load_gu(l, n):
         slot = n % 2
@@ -104,6 +107,53 @@
         cols = pl.ds(pl.multiple_of(me * FCOLS + n * CW, 128), CW)
         pltpu.make_async_copy(wg_in.at[l, :, cols], wgu.at[slot, mine, pl.ds(0, CW)], ld_sem.at[1 + slot]).start()
         pltpu.make_async_copy(wu_in.at[l, :, cols], wgu.at[slot, mine, pl.ds(CW, CW)], ld_sem.at[1 + slot]).start()
+
+    def relayout(l):
+        def fetch(i):
+            slot = i % 2
+            rows = pl.ds(pl.multiple_of(i * RB, RB), RB)
+            return [pltpu.make_async_copy(src.at[l, rows], dst.at[slot], rl_in.at[slot, k])
+                    for k, (src, dst) in enumerate(((wq_in, rq), (wk_in, rk), (wv_in, rv)))]
+
+        def put(i):
+            slot = i % 2
+            rows = pl.ds(pl.multiple_of(i * RB, RB), RB)
+            return pltpu.make_async_copy(st.at[slot], stage_qkv.at[l, :, rows, :], rl_out.at[slot])
+
+        steps = ROWS // RB
+        for cp in fetch(0):
+            cp.start()
+
+        def step(i, carry):
+            slot = i % 2
+
+            @pl.when(i + 1 < steps)
+            def _():
+                for cp in fetch(i + 1):
+                    cp.start()
+            for cp in fetch(i):
+                cp.wait()
+
+            @pl.when(i >= 2)
+            def _():
+                put(i - 2).wait()
+
+            def block(b, carry):
+                rows = pl.ds(pl.multiple_of(b * 16, 16), 16)
+                q = rq[slot, rows].astype(F32).reshape(16, DEV * QCOLS).astype(BF16)
+                k = rk[slot, rows].astype(F32).reshape(16, DEV * HD).astype(BF16)
+                v = rv[slot, rows].astype(F32).reshape(16, DEV * HD).astype(BF16)
+                for e in range(DEV):
+                    st[slot, e, rows, :QCOLS] = q[:, e * QCOLS:(e + 1) * QCOLS]
+                    st[slot, e, rows, QCOLS:QCOLS + HD] = k[:, e * HD:(e + 1) * HD]
+                    st[slot, e, rows, QCOLS + HD:] = v[:, e * HD:(e + 1) * HD]
+                return carry
+            lax.fori_loop(0, RB // 16, block, 0)
+            put(i).start()
+            return carry
+        lax.fori_loop(0, steps, step, 0)
+        put(steps - 2).wait()
+        put(steps - 1).wait()
 
     my_slot = c * CHIPS + chip
 
@@ -155,82 +205,71 @@
         for k in (6, 7, 8, 9):
             u_copy(my_slot, None, k, mate).wait_send()
 
-    def reduce_scatter(lhs, rhs, after_stage1, after_stage2):
+    def reduce_scatter(lhs, rhs, after_stage2):
         own, other = c * CHIPS, (1 - c) * CHIPS
         order = ((chip_d, chip_x, chip_y, chip), (chip_d, chip_y, chip_x, chip))
         first = (xn, yn)
         second = (yn, xn)
-        TN = 512
-
-        def hcols(h):
-            return pl.ds(h * HALF, HALF)
-
-        def mate_copy(h, k):
-            return remote(part.at[other + order[h][k], :, hcols(h)], rm.at[order[h][k], :, hcols(h)],
-                          mt_s.at[h, k], mt_r.at[h, k], mate)
-
-        def stage1(h, k):
-            return remote(part.at[own + order[h][k], :, hcols(h)], r1.at[h, k], r1_s.at[h, k], r1_r.at[h, k], first[h])
-
-        def stage2(h):
-            return remote(part.at[own + order[h][2], :, hcols(h)], r2.at[h], r2_s.at[h], r2_r.at[h], second[h])
-
-        def fold(h, k, extra):
-            j = order[h][k]
+
+        def cols(p):
+            return slice(p * PW, (p + 1) * PW)
+
+        def mate_copy(p, k):
+            j = order[p % 2][k]
+            return remote(part.at[other + j, :, pl.ds(p * PW, PW)], rm.at[j, :, pl.ds(p * PW, PW)], mt_s.at[p, k], mt_r.at[p, k], mate)
+
+        def stage1(p, k):
+            return remote(part.at[own + order[p % 2][k], :, pl.ds(p * PW, PW)], r1.at[p, k], r1_s.at[p, k], r1_r.at[p, k], first[p % 2])
+
+        def stage2(p):
+            return remote(part.at[own + order[p % 2][2], :, pl.ds(p * PW, PW)], r2.at[p], r2_s.at[p], r2_r.at[p], second[p % 2])
+
+        def fold(p, k, extra):
+            j = order[p % 2][k]
 
             def one(i, carry):
-                rows = pl.ds(pl.multiple_of(i * 8, 8), 8)
-                total = part[own + j, rows, hcols(h)] + rm[j, rows, hcols(h)]
+                rows = pl.ds(pl.multiple_of(i * 16, 16), 16)
+                total = part[own + j, rows, cols(p)] + rm[j, rows, cols(p)]
                 if extra is not None:
                     total = total + extra[rows, :]
-                part[own + j, rows, hcols(h)] = total
+                part[own + j, rows, cols(p)] = total
                 return carry
-            lax.fori_loop(0, SEQ // 8, one, 0)
-
-        for h in range(2):
+            lax.fori_loop(0, SEQ // 16, one, 0)
+
+        for p in range(NP):
             for grp in (other, own):
-                a = lhs(grp)
-
-                def tile(t, carry, grp=grp, h=h, a=a):
-                    cols = pl.ds(pl.multiple_of(h * HALF + t * TN, TN), TN)
-                    prod = jnp.dot(a, rhs[:, cols], preferred_element_type=F32)
-                    part[pl.ds(grp, CHIPS), :, cols] = prod.reshape(CHIPS, SEQ, TN)
-                    return carry
-                lax.fori_loop(0, HALF // TN, tile, 0)
+                prod = jnp.dot(lhs(grp), rhs[:, cols(p)], preferred_element_type=F32)
+                part[pl.ds(grp, CHIPS), :, cols(p)] = prod.reshape(CHIPS, SEQ, PW)
                 if grp is other:
                     for k in range(4):
-                        mate_copy(h, k).start()
+                        mate_copy(p, k).start()
             for k in (0, 1):
-                mate_copy(h, k).wait_recv()
-                fold(h, k, None)
-                stage1(h, k).start()
-        after_stage1()
-        for h in range(2):
-            mate_copy(h, 2).wait_recv()
-            stage1(h, 0).wait_recv()
-            fold(h, 2, r1.at[h, 0])
-            stage2(h).start()
+                mate_copy(p, k).wait_recv()
+                fold(p, k, None)
+                stage1(p, k).start()
+        for p in range(NP):
+            mate_copy(p, 2).wait_recv()
+            stage1(p, 0).wait_recv()
+            fold(p, 2, r1.at[p, 0])
+            stage2(p).start()
         after_stage2()
-        for h in range(2):
-            mate_copy(h, 3).wait_recv()
-            stage1(h, 1).wait_recv()
-            stage2(h).wait_recv()
-
-            def last(i, carry, h=h):
+        for p in range(NP):
+            mate_copy(p, 3).wait_recv()
+            stage1(p, 1).wait_recv()
+            stage2(p).wait_recv()
+
+            def last(i, carry, p=p):
                 rows = pl.ds(pl.multiple_of(i * 16, 16), 16)
-                total = (part[own + chip, rows, hcols(h)] + rm[chip, rows, hcols(h)]) + (r1[h, 1, rows, :] + r2[h, rows, :])
-                xb[rows, hcols(h)] = (xb[rows, hcols(h)].astype(F32) + total).astype(BF16)
+                total = (part[own + chip, rows, cols(p)] + rm[chip, rows, cols(p)]) + (r1[p, 1, rows, :] + r2[p, rows, :])
+                xb[rows, cols(p)] = (xb[rows, cols(p)].astype(F32) + total).astype(BF16)
                 return carry
             lax.fori_loop(0, SEQ // 16, last, 0)
-        for h in range(2):
+        for p in range(NP):
             for k in range(4):
-                mate_copy(h, k).wait_send()
+                mate_copy(p, k).wait_send()
             for k in range(2):
-                stage1(h, k).wait_send()
-            stage2(h).wait_send()
-
-    def nothing():
-        pass
+                stage1(p, k).wait_send()
+            stage2(p).wait_send()
 
     own_x = pltpu.make_async_copy(x_in, xb, l_sem.at[2])
     own_x.start()
@@ -238,7 +277,7 @@
         remote(g_in, gains.at[me], s_gain.at[0], s_gain.at[1], dev(*f)).start()
     own_g = pltpu.make_async_copy(g_in, gains.at[me], l_sem.at[3])
     own_g.start()
-    send_qkv(0)
+    send_gu(0, 0)
     own_x.wait()
     own_g.wait()
     bytes_wait(gains.at[pl.ds(0, DEV - 1)], s_gain.at[1])
@@ -251,8 +290,19 @@
         ld_d.start()
         norm(2 * l)
         gather_start()
+
+        @pl.when(l == 0)
+        def _():
+            relayout(0)
+            send_qkv(0)
+
         gather_forward()
-        send_gu(l, 0)
+        send_gu(l, 1)
+
+        @pl.when(l == 0)
+        def _():
+            relayout(1)
+
         bytes_wait(land_qkv.at[l, pl.ds(0, OTHER), :], rs_qkv.at[l])
         load_qkv(l)
         gather_finish()
@@ -289,7 +339,7 @@
 
         ld_o.wait()
         reduce_scatter(lambda grp: ob[pl.ds(grp, CHIPS)].reshape(CHIPS * SEQ, QCOLS), wo,
-                       lambda: send_gu(l, 1), lambda: send_gu(l, 2))
+                       lambda: send_gu(l, 2))
 
         norm(2 * l + 1)
         gather_start()
@@ -320,8 +370,13 @@
                 bytes_wait(land_gu.at[l, n + 2, pl.ds(0, OTHER), :], rs_gu.at[l, n + 2])
                 load_gu(l, n + 2)
 
+        def next_chunk():
+            @pl.when(l + 1 < LAYERS)
+            def _():
+                send_gu(l + 1, 0)
+
         ld_d.wait()
-        reduce_scatter(lambda grp: zb[pl.ds(grp, CHIPS)].reshape(CHIPS * SEQ, FCOLS), wd, nothing, nothing)
+        reduce_scatter(lambda grp: zb[pl.ds(grp, CHIPS)].reshape(CHIPS * SEQ, FCOLS), wd, next_chunk)
 
         bytes_wait(land_qkv.at[l, pl.ds(0, OTHER), :], ss_qkv.at[l])
         for n in range(NCH):
@@ -344,8 +399,6 @@
     def local_forward(hidden, attn_norm, w_q, w_k, w_v, w_o, mlp_norm, w_gate, w_up, w_down):
         gains = jnp.stack([attn_norm[0], mlp_norm[0], attn_norm[1], mlp_norm[1]]).astype(F32)
         gains = jnp.pad(gains, ((0, 4), (0, 0)))
-        wqkv = jnp.concatenate([w_q.reshape(LAYERS, ROWS, DEV, QCOLS), w_k.reshape(LAYERS, ROWS, DEV, HD),
-                                w_v.reshape(LAYERS, ROWS, DEV, HD)], axis=-1).reshape(LAYERS, ROWS, DEV * QKV)
         hbm = pl.BlockSpec(memory_space=pltpu.HBM)
         vmem = pl.BlockSpec(memory_space=pltpu.VMEM)
         dma = pltpu.SemaphoreType.DMA
@@ -353,17 +406,22 @@
             body,
             name="two_layers",
             out_shape=(jax.ShapeDtypeStruct((SEQ, DIM), BF16),
+                       jax.ShapeDtypeStruct((LAYERS, DEV, ROWS, QKV), BF16),
                        jax.ShapeDtypeStruct((LAYERS, DIM, QKV), BF16),
                        jax.ShapeDtypeStruct((LAYERS, NCH, DIM, 2 * CW), BF16)),
-            in_specs=[hbm, vmem, vmem, vmem, hbm, hbm, hbm, hbm, hbm],
-            out_specs=(hbm, hbm, hbm),
+            in_specs=[hbm, vmem, vmem, vmem, hbm, hbm, hbm, hbm, hbm, hbm, hbm],
+            out_specs=(hbm, hbm, hbm, hbm),
             scratch_shapes=[
+                pltpu.VMEM((2, RB, DEV * QH, HD), BF16),
+                pltpu.VMEM((2, RB, DEV, HD), BF16),
+                pltpu.VMEM((2, RB, DEV, HD), BF16),
+                pltpu.VMEM((2, DEV, RB, QKV), BF16),
                 pltpu.VMEM((SEQ, DIM), BF16),
                 pltpu.VMEM((DEV, SEQ, DIM), BF16),
                 pltpu.VMEM((DEV, SEQ, DIM), F32),
                 pltpu.VMEM((CHIPS, SEQ, DIM), F32),
-                pltpu.VMEM((2, 2, SEQ, HALF), F32),
-                pltpu.VMEM((2, SEQ, HALF), F32),
+                pltpu.VMEM((NP, 2, SEQ, PW), F32),
+                pltpu.VMEM((NP, SEQ, PW), F32),
                 pltpu.VMEM((DIM, QKV), BF16),
                 pltpu.VMEM((QCOLS, DIM), BF16),
                 pltpu.VMEM((FCOLS, DIM), BF16),
@@ -375,10 +433,11 @@
                 pltpu.VMEM((DEV, SEQ, FCOLS), BF16),
                 pltpu.VMEM((DEV, 8, ROWS), F32),
                 dma((LAYERS,)), dma((LAYERS,)), dma((LAYERS, NCH)), dma((LAYERS, NCH)), dma((2,)), dma((4,)), dma((3,)),
-                dma((10,)), dma((10,)), dma((2, 4)), dma((2, 4)), dma((2, 2)), dma((2, 2)), dma((2,)), dma((2,)),
+                dma((2, 3)), dma((2,)),
+                dma((10,)), dma((10,)), dma((NP, 4)), dma((NP, 4)), dma((NP, 2)), dma((NP, 2)), dma((NP,)), dma((NP,)),
             ],
             compiler_params=pltpu.CompilerParams(collective_id=0, has_side_effects=True, vmem_limit_bytes=66_000_000),
-        )(hidden[0], gains, cos, sin, wqkv, w_o, w_gate, w_up, w_down)[0]
+        )(hidden[0], gains, cos, sin, w_q, w_k, w_v, w_o, w_gate, w_up, w_down)[0]
         return out[None]
 
     return jax.shard_map(local_forward, mesh=mesh, in_specs=(batch_spec, gain_spec, proj_spec, proj_spec, proj_spec, mat_spec, gain_spec, mat_spec, mat_spec, mat_spec), out_specs=batch_spec, check_vma=False)

time: 732 us -> 691 us (0.944)
  local copies, waits for them, and re-layouts: 23.6 us -> 2.83 us
  Pallas kernels: 701 us -> 687 us
    reshape x2 -> x0, local copies, waits for them, and re-layouts: 20.7 us -> none  [the longest x1 12.3 us: local_forward(): wqkv = jnp.concatenate([w_q.reshape(LAYERS, ROWS, DEV, QCOLS), w_k.reshap...]
    pallas_call x1, Pallas kernels: 701 us -> 687 us  [local_forward(): pl.pallas_call(body, name='two_layers', out_shape=(jax.ShapeDtypeStruct((...]
where the time goes in v2:
time: 691 us
  Pallas kernels  687 us (99%)
    pallas_call x1, Pallas kernels, local_forward(): pl.pallas_call(body, name='two_layers', out_shape=(jax.ShapeDtypeStruct((...  687 us

profile of v2, /device:TPU:0, one launch (start us, length us, event | category | flops | bytes accessed | tf_op | source)
XLA Modules:
  0.0 690.6 jit_solution(11175644157899547070)
XLA Ops:
  0.0 0.8 fusion.8
  0.8 0.6 fusion.7.g_in
  1.4 687.2 %two_layers.1 = (bf16[128,3072]{1,0:T(8,128)(2,1)}, bf16[2,8,384,640]{3,2,1,0:T(8,128)(2,1)}, bf16[2,3072,640]{2,1,0:T(8,128)(2,1)}, bf16[2,4,3072,512]{3,2,1,0:T(8,128)(2,1)}) custom-call(bf16[128,3072]{1,0:T(8,128)(2,1)} %bitcast.3, f32[8,384]{1,0:T(8,128)} %fusion.7.g_in, f32[128,128]{1,0:T(8,128)} %constant.8.clone.cos_in, ...), custom_call_target="tpu_custom_call" | custom-call | tf_op jit(solution)/shard_map/two_layers/pallas_call | solution.py:405
  688.6 2.1 copy.14

commit v3 on v2

--- a/solution.py
+++ b/solution.py
@@ -26,8 +26,13 @@
 QKV = QCOLS + 2 * HD
 FFN = 8192
 FCOLS = FFN // DEV
-NCH = 4
-CW = FCOLS // NCH
+PAIR = 2 * ROWS
+CHUNKS = ((0, 256), (256, 256), (512, 128), (640, 256), (896, 128))
+NCH = len(CHUNKS)
+LAST = NCH - 1
+SLOT = (0, 1, 0, 1)
+WIDE = 512
+KPRE = CHUNKS[LAST][0]
 LAYERS = 2
 RB = 96
 NP = 4
@@ -42,9 +47,9 @@
     return np.concatenate([cos, cos], axis=1), np.concatenate([-sin, sin], axis=1)
 
 
-def body(x_in, g_in, cos_in, sin_in, wq_in, wk_in, wv_in, wo_in, wg_in, wu_in, wd_in,
+def body(x_in, ga_in, gm_in, cos_in, sin_in, wq_in, wk_in, wv_in, wo_in, wg_in, wu_in, wd_in,
          out, stage_qkv, land_qkv, land_gu,
-         rq, rk, rv, st, xb, u, part, rm, r1, r2, wqkv, wo, wd, wgu, qb, kb, vb, ob, zb, gains,
+         rq, rk, rv, st, xb, u, part, rm, r1, r2, wqkv, wo, wd, wgu, wlast, lsum, qb, kb, vb, ob, zb, ga, gm, cos_t, sin_t,
          ss_qkv, rs_qkv, ss_gu, rs_gu, s_gain, l_sem, ld_sem,
          rl_in, rl_out, ag_s, ag_r, mt_s, mt_r, r1_s, r1_r, r2_s, r2_r):
     me = lax.axis_index("fsdp")
@@ -61,7 +66,7 @@
 
     mate, xn, yn = dev(0, 0, 1), dev(0, 1, 0), dev(1, 0, 0)
     chip_x, chip_y, chip_d = xn // 2, yn // 2, dev(1, 1, 0) // 2
-    flips = ((1, 1, 0), (1, 1, 1), (0, 1, 0), (1, 0, 0), (0, 1, 1), (1, 0, 1), (0, 0, 1))
+    flips = ((0, 1, 0), (1, 0, 0), (0, 1, 1), (1, 0, 1), (1, 1, 0), (1, 1, 1), (0, 0, 1))
 
     def remote(src, dst, ssem, rsem, target):
         return pltpu.make_async_remote_copy(src, dst, ssem, rsem, device_id={"fsdp": target}, device_id_type=MESH)
@@ -82,12 +87,21 @@
                    ss_qkv.at[l], rs_qkv.at[l], e).start()
 
     def send_gu(l, n):
+        off, w = CHUNKS[n]
+        rows = pl.ds(pl.multiple_of(me * ROWS, ROWS), ROWS)
         for f in flips:
             e = dev(*f)
-            cols = pl.ds(pl.multiple_of(e * FCOLS + n * CW, 128), CW)
-            rows = pl.ds(pl.multiple_of(me * ROWS, ROWS), ROWS)
-            remote(wg_in.at[l, :, cols], land_gu.at[l, n, rows, pl.ds(0, CW)], ss_gu.at[l, n], rs_gu.at[l, n], e).start()
-            remote(wu_in.at[l, :, cols], land_gu.at[l, n, rows, pl.ds(CW, CW)], ss_gu.at[l, n], rs_gu.at[l, n], e).start()
+            cols = pl.ds(pl.multiple_of(e * FCOLS + off, 128), w)
+            for src, k in ((wg_in, 0), (wu_in, 1)):
+                dst = wlast.at[rows, pl.ds(k * w, w)] if n == LAST else land_gu.at[l, rows, pl.ds(2 * off + k * w, w)]
+                got = n + 1 if n == LAST and f[0] and f[1] else n
+                remote(src.at[l, :, cols], dst, ss_gu.at[l, n], rs_gu.at[l, got], e).start()
+
+    def gu_bytes(l, n):
+        off, w = CHUNKS[n]
+        if n == LAST:
+            return wlast.at[pl.ds(0, OTHER), :]
+        return land_gu.at[l, pl.ds(0, OTHER), pl.ds(2 * off, 2 * w)]
 
     OTHER = (DEV - 1) * ROWS
 
@@ -98,15 +112,20 @@
         mine = pl.ds(pl.multiple_of(me * ROWS, ROWS), ROWS)
         pltpu.make_async_copy(stage_qkv.at[l, me], wqkv.at[mine, :], ld_sem.at[0]).start()
 
+    def own_gu(l, n):
+        off, w = CHUNKS[n]
+        mine = pl.ds(pl.multiple_of(me * ROWS, ROWS), ROWS)
+        cols = pl.ds(pl.multiple_of(me * FCOLS + off, 128), w)
+        for src, k in ((wg_in, 0), (wu_in, 1)):
+            dst = wlast.at[mine, pl.ds(k * w, w)] if n == LAST else wgu.at[SLOT[n], mine, pl.ds(k * w, w)]
+            pltpu.make_async_copy(src.at[l, :, cols], dst, ld_sem.at[1 + n]).start()
+
     def load_gu(l, n):
-        slot = n % 2
+        off, w = CHUNKS[n]
         for f in flips:
             rows = pl.ds(pl.multiple_of(dev(*f) * ROWS, ROWS), ROWS)
-            pltpu.make_async_copy(land_gu.at[l, n, rows, :], wgu.at[slot, rows, :], ld_sem.at[1 + slot]).start()
-        mine = pl.ds(pl.multiple_of(me * ROWS, ROWS), ROWS)
-        cols = pl.ds(pl.multiple_of(me * FCOLS + n * CW, 128), CW)
-        pltpu.make_async_copy(wg_in.at[l, :, cols], wgu.at[slot, mine, pl.ds(0, CW)], ld_sem.at[1 + slot]).start()
-        pltpu.make_async_copy(wu_in.at[l, :, cols], wgu.at[slot, mine, pl.ds(CW, CW)], ld_sem.at[1 + slot]).start()
+            pltpu.make_async_copy(land_gu.at[l, rows, pl.ds(2 * off, 2 * w)], wgu.at[SLOT[n], rows, pl.ds(0, 2 * w)], ld_sem.at[1 + n]).start()
+        own_gu(l, n)
 
     def relayout(l):
         def fetch(i):
@@ -157,14 +176,15 @@
 
     my_slot = c * CHIPS + chip
 
-    def norm(row):
+    def norm(gains, l):
         def one(i, carry):
             rows = pl.ds(pl.multiple_of(i * 16, 16), 16)
             wide = xb[rows, :].astype(F32)
             inv = lax.rsqrt(jnp.mean(wide * wide, axis=-1, keepdims=True) + NORM_EPS)
             for s in range(DEV):
                 cols = slice(s * ROWS, (s + 1) * ROWS)
-                g = gains[s, pl.ds(row, 1), :]
+                both = gains[s].astype(F32)
+                g = jnp.where(l == 0, both[0:1], both[1:2])
                 u[my_slot, rows, cols] = (wide[:, cols] * inv * g).astype(BF16)
             return carry
         lax.fori_loop(0, SEQ // 16, one, 0)
@@ -205,7 +225,7 @@
         for k in (6, 7, 8, 9):
             u_copy(my_slot, None, k, mate).wait_send()
 
-    def reduce_scatter(lhs, rhs, after_stage2):
+    def reduce_scatter(act, rhs, k0, between, then):
         own, other = c * CHIPS, (1 - c) * CHIPS
         order = ((chip_d, chip_x, chip_y, chip), (chip_d, chip_y, chip_x, chip))
         first = (xn, yn)
@@ -236,24 +256,42 @@
                 return carry
             lax.fori_loop(0, SEQ // 16, one, 0)
 
+        def products(p, grp, ks):
+            slots = [grp + order[p % 2][k] for k in ks]
+            a = jnp.concatenate([act[slot, :, k0:] for slot in slots], axis=0)
+            prod = jnp.dot(a, rhs[k0:, cols(p)], preferred_element_type=F32)
+            for i, slot in enumerate(slots):
+                term = prod[i * SEQ:(i + 1) * SEQ]
+                part[slot, :, cols(p)] = part[slot, :, cols(p)] + term if k0 else term
+
+        for pair in range(NP // 2):
+            both = (2 * pair, 2 * pair + 1)
+            for p in both:
+                products(p, other, (0, 1))
+                for k in (0, 1):
+                    mate_copy(p, k).start()
+            if pair == 0 and between is not None:
+                between()
+            for p in both:
+                products(p, own, (0, 1))
+            for k in (0, 1):
+                for p in both:
+                    mate_copy(p, k).wait_recv()
+                    fold(p, k, None)
+                    stage1(p, k).start()
         for p in range(NP):
-            for grp in (other, own):
-                prod = jnp.dot(lhs(grp), rhs[:, cols(p)], preferred_element_type=F32)
-                part[pl.ds(grp, CHIPS), :, cols(p)] = prod.reshape(CHIPS, SEQ, PW)
-                if grp is other:
-                    for k in range(4):
-                        mate_copy(p, k).start()
-            for k in (0, 1):
-                mate_copy(p, k).wait_recv()
-                fold(p, k, None)
-                stage1(p, k).start()
+            products(p, other, (2, 3))
+            for k in (2, 3):
+                mate_copy(p, k).start()
+            products(p, own, (2, 3))
         for p in range(NP):
             mate_copy(p, 2).wait_recv()
             stage1(p, 0).wait_recv()
             fold(p, 2, r1.at[p, 0])
             stage2(p).start()
-        after_stage2()
         for p in range(NP):
+            if p == NP // 2:
+                then()
             mate_copy(p, 3).wait_recv()
             stage1(p, 1).wait_recv()
             stage2(p).wait_recv()
@@ -271,24 +309,25 @@
                 stage1(p, k).wait_send()
             stage2(p).wait_send()
 
-    own_x = pltpu.make_async_copy(x_in, xb, l_sem.at[2])
-    own_x.start()
-    for f in flips:
-        remote(g_in, gains.at[me], s_gain.at[0], s_gain.at[1], dev(*f)).start()
-    own_g = pltpu.make_async_copy(g_in, gains.at[me], l_sem.at[3])
-    own_g.start()
+    for src, dst, k in ((ga_in, ga, 0), (gm_in, gm, 1)):
+        for f in flips:
+            remote(src, dst.at[me], s_gain.at[k], s_gain.at[2 + k], dev(*f)).start()
     send_gu(0, 0)
-    own_x.wait()
-    own_g.wait()
-    bytes_wait(gains.at[pl.ds(0, DEV - 1)], s_gain.at[1])
-    bytes_wait(gains.at[pl.ds(0, DEV - 1)], s_gain.at[0])
+    starts = [pltpu.make_async_copy(src, dst, l_sem.at[2 + k]) for k, (src, dst) in enumerate(
+        ((x_in, xb), (ga_in, ga.at[me]), (gm_in, gm.at[me]), (cos_in, cos_t), (sin_in, sin_t)))]
+    for cp in starts:
+        cp.start()
+    for cp in starts:
+        cp.wait()
+    bytes_wait(ga.at[pl.ds(0, DEV - 1)], s_gain.at[2])
+    bytes_wait(gm.at[pl.ds(0, DEV - 1)], s_gain.at[3])
 
     def layer(l, carry):
         ld_o = pltpu.make_async_copy(wo_in.at[l], wo, l_sem.at[0])
         ld_d = pltpu.make_async_copy(wd_in.at[l], wd, l_sem.at[1])
         ld_o.start()
         ld_d.start()
-        norm(2 * l)
+        norm(ga, l)
         gather_start()
 
         @pl.when(l == 0)
@@ -310,7 +349,7 @@
 
         def qkv_block(i, carry):
             prod = jnp.dot(u[pl.ds(i * 2, 2)].reshape(2 * SEQ, DIM), wqkv[...], preferred_element_type=F32)
-            cos, sin = cos_in[...], sin_in[...]
+            cos, sin = cos_t[...], sin_t[...]
             for s in range(2):
                 rows = slice(s * SEQ, (s + 1) * SEQ)
                 for h in range(QH + 1):
@@ -338,55 +377,96 @@
         lax.fori_loop(0, DEV, attend, 0)
 
         ld_o.wait()
-        reduce_scatter(lambda grp: ob[pl.ds(grp, CHIPS)].reshape(CHIPS * SEQ, QCOLS), wo,
-                       lambda: send_gu(l, 2))
-
-        norm(2 * l + 1)
+        reduce_scatter(ob, wo, 0, None, lambda: send_gu(l, 2))
+
+        norm(gm, l)
         gather_start()
         gather_forward()
         send_gu(l, 3)
-        for n in range(2):
-            bytes_wait(land_gu.at[l, n, pl.ds(0, OTHER), :], rs_gu.at[l, n])
-            load_gu(l, n)
-        gather_finish()
+        send_gu(l, LAST)
 
         @pl.when(l + 1 < LAYERS)
         def _():
             send_qkv(l + 1)
 
-        for n in range(NCH):
-            slot = n % 2
-            bytes_wait(wgu.at[slot], ld_sem.at[1 + slot])
-
-            def mlp_block(i, carry, n=n, slot=slot):
-                prod = jnp.dot(u[pl.ds(i * 4, 4)].reshape(4 * SEQ, DIM), wgu[slot], preferred_element_type=F32)
-                gate = prod[:, :CW].astype(BF16).astype(F32)
-                up = prod[:, CW:].astype(BF16).astype(F32)
-                z = (gate * jax.nn.sigmoid(gate) * up).astype(BF16)
-                zb[pl.ds(i * 4, 4), :, n * CW:(n + 1) * CW] = z.reshape(4, SEQ, CW)
+        def chunk_arrives(n):
+            bytes_wait(gu_bytes(l, n), rs_gu.at[l, n])
+            load_gu(l, n)
+
+        chunk_arrives(0)
+        chunk_arrives(1)
+        own_gu(l, LAST)
+        gather_finish()
+
+        def activate(prod, n, i):
+            off, w = CHUNKS[n]
+            gate = prod[:, :w].astype(BF16).astype(F32)
+            up = prod[:, w:].astype(BF16).astype(F32)
+            z = (gate * jax.nn.sigmoid(gate) * up).astype(BF16)
+            zb[pl.ds(i * CHIPS, CHIPS), :, off:off + w] = z.reshape(CHIPS, SEQ, w)
+
+        def mlp_block(n, i):
+            rows = u[pl.ds(i * CHIPS, CHIPS)].reshape(CHIPS * SEQ, DIM)
+            activate(jnp.dot(rows, wgu[SLOT[n], :, :2 * CHUNKS[n][1]], preferred_element_type=F32), n, i)
+
+        def last_term(i, k):
+            depth = pl.ds(pl.multiple_of(k * PAIR, PAIR), PAIR)
+            rows = u[pl.ds(i * CHIPS, CHIPS), :, depth].reshape(CHIPS * SEQ, PAIR)
+            return jnp.dot(rows, wlast[depth, :], preferred_element_type=F32)
+
+        def last_near(i, carry):
+            lsum[i] = (last_term(i, chip) + last_term(i, chip_x)) + last_term(i, chip_y)
+            return carry
+
+        def last_block(i):
+            activate(lsum[i] + last_term(i, chip_d), LAST, i)
+
+        def mlp_chunk(n):
+            bytes_wait(wgu.at[SLOT[n], :, pl.ds(0, 2 * CHUNKS[n][1])], ld_sem.at[1 + n])
+
+            def block(i, carry):
+                mlp_block(n, i)
                 return carry
-            lax.fori_loop(0, 2, mlp_block, 0)
-            if n + 2 < NCH:
-                bytes_wait(land_gu.at[l, n + 2, pl.ds(0, OTHER), :], rs_gu.at[l, n + 2])
-                load_gu(l, n + 2)
+            lax.fori_loop(0, 2, block, 0)
+
+        mlp_chunk(0)
+        chunk_arrives(2)
+        mlp_chunk(1)
+        mlp_chunk(2)
+        chunk_arrives(3)
+        mlp_chunk(3)
+        ld_d.wait()
+
+        def before_last(i, carry):
+            slots = pl.ds(i * CHIPS, CHIPS)
+            z = zb[slots, :, :KPRE].reshape(CHIPS * SEQ, KPRE)
+            for p in range(NP):
+                prod = jnp.dot(z, wd[:KPRE, p * PW:(p + 1) * PW], preferred_element_type=F32)
+                part[slots, :, p * PW:(p + 1) * PW] = prod.reshape(CHIPS, SEQ, PW)
+            return carry
+        lax.fori_loop(0, 2, before_last, 0)
+        bytes_wait(wlast.at[pl.ds(0, OTHER - PAIR), :], rs_gu.at[l, LAST])
+        bytes_wait(wlast.at[pl.ds(0, ROWS), :], ld_sem.at[1 + LAST])
+        lax.fori_loop(0, 2, last_near, 0)
+        bytes_wait(wlast.at[pl.ds(0, PAIR), :], rs_gu.at[l, LAST + 1])
+        last_block(1 - c)
 
         def next_chunk():
             @pl.when(l + 1 < LAYERS)
             def _():
                 send_gu(l + 1, 0)
 
-        ld_d.wait()
-        reduce_scatter(lambda grp: zb[pl.ds(grp, CHIPS)].reshape(CHIPS * SEQ, FCOLS), wd, next_chunk)
+        reduce_scatter(zb, wd, KPRE, lambda: last_block(c), next_chunk)
 
         bytes_wait(land_qkv.at[l, pl.ds(0, OTHER), :], ss_qkv.at[l])
         for n in range(NCH):
-            bytes_wait(land_gu.at[l, n, pl.ds(0, OTHER), :], ss_gu.at[l, n])
+            bytes_wait(gu_bytes(l, n), ss_gu.at[l, n])
         return carry
 
     lax.fori_loop(0, LAYERS, layer, 0)
-    done = pltpu.make_async_copy(xb, out, l_sem.at[2])
-    done.start()
-    done.wait()
+    bytes_wait(ga.at[pl.ds(0, DEV - 1)], s_gain.at[0])
+    bytes_wait(gm.at[pl.ds(0, DEV - 1)], s_gain.at[1])
+    out[...] = xb[...]
 
 
 def solution(mesh):
@@ -397,20 +477,18 @@
     cos, sin = rope_tables()
 
     def local_forward(hidden, attn_norm, w_q, w_k, w_v, w_o, mlp_norm, w_gate, w_up, w_down):
-        gains = jnp.stack([attn_norm[0], mlp_norm[0], attn_norm[1], mlp_norm[1]]).astype(F32)
-        gains = jnp.pad(gains, ((0, 4), (0, 0)))
         hbm = pl.BlockSpec(memory_space=pltpu.HBM)
         vmem = pl.BlockSpec(memory_space=pltpu.VMEM)
         dma = pltpu.SemaphoreType.DMA
         out = pl.pallas_call(
             body,
             name="two_layers",
-            out_shape=(jax.ShapeDtypeStruct((SEQ, DIM), BF16),
+            out_shape=(pltpu.VMEM((SEQ, DIM), BF16),
                        jax.ShapeDtypeStruct((LAYERS, DEV, ROWS, QKV), BF16),
                        jax.ShapeDtypeStruct((LAYERS, DIM, QKV), BF16),
-                       jax.ShapeDtypeStruct((LAYERS, NCH, DIM, 2 * CW), BF16)),
-            in_specs=[hbm, vmem, vmem, vmem, hbm, hbm, hbm, hbm, hbm, hbm, hbm],
-            out_specs=(hbm, hbm, hbm, hbm),
+                       jax.ShapeDtypeStruct((LAYERS, DIM, 2 * FCOLS), BF16)),
+            in_specs=[hbm] * 12,
+            out_specs=(vmem, hbm, hbm, hbm),
             scratch_shapes=[
                 pltpu.VMEM((2, RB, DEV * QH, HD), BF16),
                 pltpu.VMEM((2, RB, DEV, HD), BF16),
@@ -425,19 +503,24 @@
                 pltpu.VMEM((DIM, QKV), BF16),
                 pltpu.VMEM((QCOLS, DIM), BF16),
                 pltpu.VMEM((FCOLS, DIM), BF16),
-                pltpu.VMEM((2, DIM, 2 * CW), BF16),
+                pltpu.VMEM((2, DIM, WIDE), BF16),
+                pltpu.VMEM((DIM, 2 * CHUNKS[LAST][1]), BF16),
+                pltpu.VMEM((2, CHIPS * SEQ, 2 * CHUNKS[LAST][1]), F32),
                 pltpu.VMEM((DEV, QH * SEQ, HD), BF16),
                 pltpu.VMEM((DEV, SEQ, HD), BF16),
                 pltpu.VMEM((DEV, SEQ, HD), BF16),
                 pltpu.VMEM((DEV, SEQ, QCOLS), BF16),
                 pltpu.VMEM((DEV, SEQ, FCOLS), BF16),
-                pltpu.VMEM((DEV, 8, ROWS), F32),
-                dma((LAYERS,)), dma((LAYERS,)), dma((LAYERS, NCH)), dma((LAYERS, NCH)), dma((2,)), dma((4,)), dma((3,)),
+                pltpu.VMEM((DEV, LAYERS, ROWS), BF16),
+                pltpu.VMEM((DEV, LAYERS, ROWS), BF16),
+                pltpu.VMEM((SEQ, HD), F32),
+                pltpu.VMEM((SEQ, HD), F32),
+                dma((LAYERS,)), dma((LAYERS,)), dma((LAYERS, NCH)), dma((LAYERS, NCH + 1)), dma((4,)), dma((7,)), dma((1 + NCH,)),
                 dma((2, 3)), dma((2,)),
                 dma((10,)), dma((10,)), dma((NP, 4)), dma((NP, 4)), dma((NP, 2)), dma((NP, 2)), dma((NP,)), dma((NP,)),
             ],
-            compiler_params=pltpu.CompilerParams(collective_id=0, has_side_effects=True, vmem_limit_bytes=66_000_000),
-        )(hidden[0], gains, cos, sin, w_q, w_k, w_v, w_o, w_gate, w_up, w_down)[0]
+            compiler_params=pltpu.CompilerParams(collective_id=0, has_side_effects=True, vmem_limit_bytes=65_000_000),
+        )(hidden[0], attn_norm, mlp_norm, cos, sin, w_q, w_k, w_v, w_o, w_gate, w_up, w_down)[0]
         return out[None]
 
     return jax.shard_map(local_forward, mesh=mesh, in_specs=(batch_spec, gain_spec, proj_spec, proj_spec, proj_spec, mat_spec, gain_spec, mat_spec, mat_spec, mat_spec), out_specs=batch_spec, check_vma=False)

time: 691 us -> 672 us (0.973)
  Pallas kernels: 687 us -> 671 us
    pallas_call x1, Pallas kernels: 687 us -> 671 us  [local_forward(): pl.pallas_call(body, name='two_layers', out_shape=(pltpu.VMEM((SEQ, DIM),...]
where the time goes in v3:
time: 672 us
  Pallas kernels  671 us (100%)
    pallas_call x1, Pallas kernels, local_forward(): pl.pallas_call(body, name='two_layers', out_shape=(pltpu.VMEM((SEQ, DIM),...  671 us

profile of v3, /device:TPU:0, one launch (start us, length us, event | category | flops | bytes accessed | tf_op | source)
XLA Modules:
  0.0 672.2 jit_solution(3758814040021373117)
XLA Ops:
  0.0 671.3 %two_layers.1 = (bf16[128,3072]{1,0:T(8,128)(2,1)S(1)}, bf16[2,8,384,640]{3,2,1,0:T(8,128)(2,1)}, bf16[2,3072,640]{2,1,0:T(8,128)(2,1)}, bf16[2,3072,2048]{2,1,0:T(8,128)(2,1)}) custom-call(bf16[128,3072]{1,0:T(8,128)(2,1)} %bitcast.3, bf16[2,384]{1,0:T(2,128)(2,1)} %ga_in.1, bf16[2,384]{1,0:T(2,128)(2,1)} %gm_in.1, f32[128,128]{1,0:T(8,128)} %constant.4.clone.cos_in, ...), custom_call_target="tpu_custom_call" | custom-call | tf_op jit(solution)/shard_map/two_layers/pallas_call | solution.py:483
  671.3 0.9 copy.14

commit v4 on v3

v4 whole, which is shorter than its diff:
```python
import functools

import jax
import jax.numpy as jnp
import numpy as np
from jax import lax
from jax.experimental import pallas as pl
from jax.experimental.pallas import tpu as pltpu
from jax.sharding import PartitionSpec as P

ROPE_THETA = 500000.0
NORM_EPS = 1e-5
MESH = pl.DeviceIdType.MESH
F32 = jnp.float32
BF16 = jnp.bfloat16

DEV = 8
CHIPS = 4
SEQ = 128
DIM = 3072
HALF = DIM // 2
ROWS = DIM // DEV
HD = 128
QH = 3
QCOLS = QH * HD
QKV = QCOLS + 2 * HD
FFN = 8192
FCOLS = FFN // DEV
PAIR = 2 * ROWS
CHUNKS = ((0, 128), (256, 256), (512, 256), (128, 128), (768, 128), (896, 128))
NCH = len(CHUNKS)
LAST = NCH - 1
GROUPS = (((1,), 0), ((2,), 1), ((0, 3), 0), ((4,), 1))
AHEAD = 3
WIDE = 512
SPLIT = (1, 2, 3, 4)
KPRE = CHUNKS[LAST][0]
LAYERS = 2
RB = 96
NP = 4
PW = DIM // NP


def rope_tables():
    half = HD // 2
    inv_freq = np.power(np.float32(ROPE_THETA), -(np.arange(half, dtype=np.float32) * np.float32(2.0) / np.float32(HD)))
    angles = (np.arange(SEQ, dtype=np.float32)[:, None] * inv_freq.astype(np.float32)[None, :]).astype(np.float64)
    cos, sin = np.cos(angles).astype(np.float32), np.sin(angles).astype(np.float32)
    return np.concatenate([cos, cos], axis=1), np.concatenate([-sin, sin], axis=1)


def body(x_in, ga_in, gm_in, cos_in, sin_in, wq_in, wk_in, wv_in, wo_in, wg_in, wu_in, wd_in,
         out, stage_qkv, land_qkv, land_gu, land_wo,
         rq, rk, rv, st, xcol, u, part, rm, r1, r2, wqkv, wo, wd, wgu, wlast, lsum, qb, kb, vb, ob, ob2, zb, ga, gm, cos_t, sin_t,
         ss_qkv, rs_qkv, ss_wo, rs_wo, oe_s, oe_r, ss_gu, rs_gu, s_gain, l_sem, ld_sem,
         rl_in, rl_out, ag_s, ag_r, mt_s, mt_r, r1_s, r1_r, r2_s, r2_r):
    me = lax.axis_index("fsdp")
    c = me % 2
    cx = (me // 2) % 2
    cy = me // 4
    chip = me // 2

    def dev(fy, fx, fc):
        yy = 1 - cy if fy else cy
        xx = 1 - cx if fx else cx
        cc = 1 - c if fc else c
        return yy * 4 + xx * 2 + cc

    mate, xn, yn = dev(0, 0, 1), dev(0, 1, 0), dev(1, 0, 0)
    dn = dev(1, 1, 0)
    chip_x, chip_y, chip_d = xn // 2, yn // 2, dn // 2
    mycols = pl.ds(pl.multiple_of(me * ROWS, 128), ROWS)

    def axes(l):
        return yn + l * (xn - yn), xn + l * (yn - xn)
    flips = ((0, 1, 0), (1, 0, 0), (0, 1, 1), (1, 0, 1), (1, 1, 0), (1, 1, 1), (0, 0, 1))

    def remote(src, dst, ssem, rsem, target):
        return pltpu.make_async_remote_copy(src, dst, ssem, rsem, device_id={"fsdp": target}, device_id_type=MESH)

    def bytes_wait(ref, sem):
        pltpu.make_async_copy(ref, ref, sem).wait()

    barrier = pltpu.get_barrier_semaphore()
    for f in flips:
        pl.semaphore_signal(barrier, inc=1, device_id={"fsdp": dev(*f)}, device_id_type=MESH)
    pl.semaphore_wait(barrier, DEV - 1)

    def targets(l, which):
        if which is None:
            return [(dev(*f), f[0] and f[1]) for f in flips]
        an, bn = axes(l)
        e = {"a": an, "b": bn, "d": dn}[which]
        return [(e, which == "d"), (e + 1 - 2 * c, which == "d")] + ([(mate, False)] if which == "b" else [])

    def send_qkv(l, which=None):
        for e, diagonal in targets(l, which):
            remote(stage_qkv.at[l, e],
                   land_qkv.at[l, pl.ds(pl.multiple_of(me * ROWS, ROWS), ROWS), :],
                   ss_qkv.at[l], rs_qkv.at[l], e).start()

    def send_wo(l):
        an = axes(l)[0]
        for k, to in ((0, an // 2), (1, chip_d)):
            remote(wo_in.at[l, :, pl.ds(pl.multiple_of(to * PAIR, 128), PAIR)], land_wo.at[l, :, pl.ds(k * PAIR, PAIR)],
                   ss_wo.at[l], rs_wo.at[l], an).start()

    def load_wo(l):
        for k, of in ((0, chip), (1, axes(l)[1] // 2)):
            pltpu.make_async_copy(wo_in.at[l, :, pl.ds(pl.multiple_of(of * PAIR, 128), PAIR)],
                                  wo.at[pl.ds(0, ROWS), pl.ds(k * PAIR, PAIR)], l_sem.at[0]).start()
        pltpu.make_async_copy(land_wo.at[l], wo.at[pl.ds(ROWS, ROWS), :], l_sem.at[0]).start()

    def send_gu(l, n, which=None):
        off, w = CHUNKS[n]
        rows = pl.ds(pl.multiple_of(me * ROWS, ROWS), ROWS)
        for e, diagonal in targets(l, which):
            cols = pl.ds(pl.multiple_of(e * FCOLS + off, 128), w)
            for src, k in ((wg_in, 0), (wu_in, 1)):
                dst = wlast.at[rows, pl.ds(k * w, w)] if n == LAST else land_gu.at[l, rows, pl.ds(2 * off + k * w, w)]
                got = n + 1 if n == LAST and diagonal else n
                remote(src.at[l, :, cols], dst, ss_gu.at[l, n], rs_gu.at[l, got], e).start()

    def gu_bytes(l, n):
        off, w = CHUNKS[n]
        if n == LAST:
            return wlast.at[pl.ds(0, OTHER), :]
        return land_gu.at[l, pl.ds(0, OTHER), pl.ds(2 * off, 2 * w)]

    OTHER = (DEV - 1) * ROWS

    def load_qkv(l):
        for f in flips:
            rows = pl.ds(pl.multiple_of(dev(*f) * ROWS, ROWS), ROWS)
            pltpu.make_async_copy(land_qkv.at[l, rows, :], wqkv.at[rows, :], ld_sem.at[0]).start()
        mine = pl.ds(pl.multiple_of(me * ROWS, ROWS), ROWS)
        pltpu.make_async_copy(stage_qkv.at[l, me], wqkv.at[mine, :], ld_sem.at[0]).start()

    def own_gu(l, n, dst_of, sem):
        off, w = CHUNKS[n]
        cols = pl.ds(pl.multiple_of(me * FCOLS + off, 128), w)
        for src, k in ((wg_in, 0), (wu_in, 1)):
            pltpu.make_async_copy(src.at[l, :, cols], dst_of(k * w, w), sem).start()

    def own_last(l):
        mine = pl.ds(pl.multiple_of(me * ROWS, ROWS), ROWS)
        own_gu(l, LAST, lambda at, w: wlast.at[mine, pl.ds(at, w)], ld_sem.at[1 + len(GROUPS)])

    def group_cols(g):
        chunks = GROUPS[g][0]
        return 2 * CHUNKS[chunks[0]][0], 2 * sum(CHUNKS[n][1] for n in chunks)

    def group_arrives(l, g):
        chunks, slot = GROUPS[g]
        first, width = group_cols(g)
        sem = ld_sem.at[1 + g]
        for n in chunks:
            bytes_wait(gu_bytes(l, n), rs_gu.at[l, n])
        for f in flips:
            rows = pl.ds(pl.multiple_of(dev(*f) * ROWS, ROWS), ROWS)
            pltpu.make_async_copy(land_gu.at[l, rows, pl.ds(first, width)], wgu.at[slot, rows, pl.ds(0, width)], sem).start()
        mine = pl.ds(pl.multiple_of(me * ROWS, ROWS), ROWS)
        for n in chunks:
            base = 2 * CHUNKS[n][0] - first
            own_gu(l, n, lambda at, w, base=base: wgu.at[slot, mine, pl.ds(base + at, w)], sem)

    def relayout(l):
        def fetch(i):
            slot = i % 2
            rows = pl.ds(pl.multiple_of(i * RB, RB), RB)
            return [pltpu.make_async_copy(src.at[l, rows], dst.at[slot], rl_in.at[slot, k])
                    for k, (src, dst) in enumerate(((wq_in, rq), (wk_in, rk), (wv_in, rv)))]

        def put(i):
            slot = i % 2
            rows = pl.ds(pl.multiple_of(i * RB, RB), RB)
            return pltpu.make_async_copy(st.at[slot], stage_qkv.at[l, :, rows, :], rl_out.at[slot])

        steps = ROWS // RB
        for cp in fetch(0):
            cp.start()

        def step(i, carry):
            slot = i % 2

            @pl.when(i + 1 < steps)
            def _():
                for cp in fetch(i + 1):
                    cp.start()
            for cp in fetch(i):
                cp.wait()

            @pl.when(i >= 2)
            def _():
                put(i - 2).wait()

            def block(b, carry):
                rows = pl.ds(pl.multiple_of(b * 16, 16), 16)
                q = rq[slot, rows].astype(F32).reshape(16, DEV * QCOLS).astype(BF16)
                k = rk[slot, rows].astype(F32).reshape(16, DEV * HD).astype(BF16)
                v = rv[slot, rows].astype(F32).reshape(16, DEV * HD).astype(BF16)
                for e in range(DEV):
                    st[slot, e, rows, :QCOLS] = q[:, e * QCOLS:(e + 1) * QCOLS]
                    st[slot, e, rows, QCOLS:QCOLS + HD] = k[:, e * HD:(e + 1) * HD]
                    st[slot, e, rows, QCOLS + HD:] = v[:, e * HD:(e + 1) * HD]
                return carry
            lax.fori_loop(0, RB // 16, block, 0)
            put(i).start()
            return carry
        lax.fori_loop(0, steps, step, 0)
        put(steps - 2).wait()
        put(steps - 1).wait()

    my_slot = c * CHIPS + chip

    def norm_all(gains, l):
        def one(i, carry):
            slot = i // (SEQ // 16)
            rows = pl.ds(pl.multiple_of((i % (SEQ // 16)) * 16, 16), 16)
            wide = u[slot, rows, :].astype(F32)
            inv = lax.rsqrt(jnp.mean(wide * wide, axis=-1, keepdims=True) + NORM_EPS)
            for s in range(DEV):
                cols = slice(s * ROWS, (s + 1) * ROWS)
                both = gains[s].astype(F32)
                g = jnp.where(l == 0, both[0:1], both[1:2])
                u[slot, rows, cols] = (wide[:, cols] * inv * g).astype(BF16)
            return carry
        lax.fori_loop(0, DEV * SEQ // 16, one, 0)

    def by_rows(who, half):
        slot = c * CHIPS + {"me": chip, "x": chip_x, "y": chip_y, "d": chip_d}[who]
        return u.at[slot] if half is None else u.at[slot, :, pl.ds(half * HALF, HALF)]

    def by_cols(who, half):
        e = {"me": me, "x": xn, "y": yn, "d": dn}[who]
        cols = pl.ds(pl.multiple_of(e * ROWS, 128), ROWS)
        return u.at[:, :, cols] if half is None else u.at[pl.ds(half * CHIPS, CHIPS), :, cols]

    def u_copy(ref, k, target):
        return remote(ref, ref, ag_s.at[k], ag_r.at[k], target)

    def gather_start(at):
        u_copy(at("me", 0), 0, xn).start()
        u_copy(at("me", 1), 1, yn).start()
        u_copy(at("me", 1), 2, xn).start()
        u_copy(at("me", 0), 3, yn).start()
        u_copy(at("me", None), 6, mate).start()

    def gather_forward(at):
        u_copy(at("x", 0), 0, xn).wait_recv()
        u_copy(at("x", 0), 4, yn).start()
        u_copy(at("y", 1), 1, yn).wait_recv()
        u_copy(at("y", 1), 5, xn).start()

    def gather_finish(at):
        u_copy(at("x", 1), 2, xn).wait_recv()
        u_copy(at("x", None), 7, mate).start()
        u_copy(at("y", 0), 3, yn).wait_recv()
        u_copy(at("y", None), 8, mate).start()
        u_copy(at("d", 0), 4, yn).wait_recv()
        u_copy(at("d", 1), 5, xn).wait_recv()
        u_copy(at("d", None), 9, mate).start()
        for k in (6, 7, 8, 9):
            u_copy(at("me", None), k, mate).wait_recv()
        for k in range(6):
            u_copy(at("me", 0), k, xn).wait_send()
        for k in (6, 7, 8, 9):
            u_copy(at("me", None), k, mate).wait_send()

    def keep(slot, total):
        new = (xcol[slot].astype(F32) + total).astype(BF16)
        xcol[slot] = new
        u[slot, :, mycols] = new

    def out_proj(l, after_exchange, after_sums):
        an, bn = axes(l)

        def o_copy(g):
            return remote(ob.at[pl.ds(g * CHIPS, CHIPS)], ob2.at[pl.ds(g * CHIPS, CHIPS)], oe_s.at[g], oe_r.at[g], an)

        def mate_copy(p, b):
            return remote(part.at[pl.ds(2 * p, 2), :, pl.ds(pl.multiple_of(b * PAIR + (1 - c) * ROWS, 128), ROWS)], rm.at[p, b],
                          mt_s.at[p, b], mt_r.at[p, b], mate)

        def sums(p):
            return remote(part.at[pl.ds(2 * p, 2), :, pl.ds(pl.multiple_of(PAIR + c * ROWS, 128), ROWS)], r1.at[p, 0],
                          r1_s.at[p, 0], r1_r.at[p, 0], bn)

        def fold(p):
            mate_copy(p, 1).wait_recv()
            for t in range(2):
                cols = pl.ds(pl.multiple_of(PAIR + c * ROWS, 128), ROWS)
                part[2 * p + t, :, cols] = part[2 * p + t, :, cols] + rm[p, 1, t]
            sums(p).start()

        for g in range(2):
            o_copy(g).start()
        after_exchange()
        for p in range(NP):
            if p % 2 == 0:
                o_copy(p // 2).wait_recv()
            a = jnp.concatenate([r[pl.ds(2 * p, 2)].reshape(2 * SEQ, QCOLS) for r in (ob, ob2)], axis=1)
            for b in (1, 0):
                prod = jnp.dot(a, wo[:, b * PAIR:(b + 1) * PAIR], preferred_element_type=F32)
                part[pl.ds(2 * p, 2), :, b * PAIR:(b + 1) * PAIR] = prod.reshape(2, SEQ, PAIR)
                mate_copy(p, b).start()
            if p:
                fold(p - 1)
        fold(NP - 1)
        after_sums()
        for p in range(NP):
            mate_copy(p, 0).wait_recv()
            sums(p).wait_recv()
            for t in range(2):
                keep(2 * p + t, (part[2 * p + t, :, pl.ds(pl.multiple_of(c * ROWS, 128), ROWS)] + rm[p, 0, t]) + r1[p, 0, t])
        for g in range(2):
            o_copy(g).wait_send()
        for p in range(NP):
            for b in range(2):
                mate_copy(p, b).wait_send()
            sums(p).wait_send()

    def reduce_scatter(rows_form, act, rhs, k0, between, then):
        own, other = c, 1 - c
        order = ((chip_d, chip_x, chip_y, chip), (chip_d, chip_y, chip_x, chip))
        first = (xn, yn)
        second = (yn, xn)

        def sub(p, j, core, t):
            if rows_form:
                return core * CHIPS + j, pl.ds(p * PW + t * ROWS, ROWS)
            return 2 * p + t, pl.ds(pl.multiple_of(j * PAIR + core * ROWS, 128), ROWS)

        def pieces(p, j, core, dst, ssem, rsem, target):
            for t in range(2):
                slot, cols = sub(p, j, core, t)
                remote(part.at[slot, :, cols], dst.at[t], ssem, rsem, target).start()

        def unit(sem):
            bytes_wait(r2.at[0], sem)

        def send_mate(p, k):
            j = order[p % 2][k]
            pieces(p, j, other, rm.at[p, j], mt_s.at[p, k], mt_r.at[p, k], mate)

        def fold(p, k, extra):
            j = order[p % 2][k]
            for t in range(2):
                slot, cols = sub(p, j, own, t)
                total = part[slot, :, cols] + rm[p, j, t]
                part[slot, :, cols] = total if extra is None else total + extra[t]

        def products(p, grp, ks):
            slots = [grp * CHIPS + order[p % 2][k] for k in ks]
            a = jnp.concatenate([act[slot, :, k0:] for slot in slots], axis=0)
            cols = slice(p * PW, (p + 1) * PW)
            prod = jnp.dot(a, rhs[k0:, cols], preferred_element_type=F32)
            for i, slot in enumerate(slots):
                part[slot, :, cols] = part[slot, :, cols] + prod[i * SEQ:(i + 1) * SEQ]

        def column_products(p, k):
            cols = pl.ds(pl.multiple_of(order[p % 2][k] * PAIR, 128), PAIR)
            slots = pl.ds(2 * p, 2)
            prod = jnp.dot(act[slots, :, k0:].reshape(2 * SEQ, FCOLS - k0), rhs[k0:, cols], preferred_element_type=F32)
            part[slots, :, cols] = part[slots, :, cols] + prod.reshape(2, SEQ, PAIR)

        for pair in range(NP // 2):
            both = (2 * pair, 2 * pair + 1)
            for p in both:
                if rows_form:
                    products(p, other, (0, 1))
                for k in (0, 1):
                    if not rows_form:
                        column_products(p, k)
                    send_mate(p, k)
            if pair == 0 and between is not None:
                between()
            if rows_form:
                for p in both:
                    products(p, own, (0, 1))
            for k in (0, 1):
                for p in both:
                    unit(mt_r.at[p, k])
                    fold(p, k, None)
                    pieces(p, order[p % 2][k], own, r1.at[p, k], r1_s.at[p, k], r1_r.at[p, k], first[p % 2])
        for p in range(NP):
            if rows_form:
                products(p, other, (2, 3))
            for k in (2, 3):
                if not rows_form:
                    column_products(p, k)
                send_mate(p, k)
            if rows_form:
                products(p, own, (2, 3))
        for p in range(NP):
            unit(mt_r.at[p, 2])
            unit(r1_r.at[p, 0])
            fold(p, 2, r1.at[p, 0])
            pieces(p, order[p % 2][2], own, r2.at[p], r2_s.at[p], r2_r.at[p], second[p % 2])
        for p in range(NP):
            if p == NP // 2:
                then()
            unit(mt_r.at[p, 3])
            unit(r1_r.at[p, 1])
            unit(r2_r.at[p])
            for t in range(2):
                slot, cols = sub(p, chip, own, t)
                total = (part[slot, :, cols] + rm[p, chip, t]) + (r1[p, 1, t] + r2[p, t])
                if rows_form:
                    out[:, cols] = total.astype(BF16)
                else:
                    keep(slot, total)
        for p in range(NP):
            for k in range(4):
                unit(mt_s.at[p, k])
            for k in range(2):
                unit(r1_s.at[p, k])
            unit(r2_s.at[p])

    def send_direct(l, which):
        for n in SPLIT:
            send_gu(l, n, which)

    for src, dst, k in ((ga_in, ga, 0), (gm_in, gm, 1)):
        for f in flips:
            remote(src, dst.at[me], s_gain.at[k], s_gain.at[2 + k], dev(*f)).start()
    send_gu(0, 0)
    starts = [pltpu.make_async_copy(src, dst, l_sem.at[2 + k]) for k, (src, dst) in enumerate(
        ((x_in, u.at[my_slot]), (ga_in, ga.at[me]), (gm_in, gm.at[me]), (cos_in, cos_t), (sin_in, sin_t)))]
    for cp in starts:
        cp.start()
    for cp in starts:
        cp.wait()
    gather_start(by_rows)
    relayout(0)
    gather_forward(by_rows)
    send_qkv(0)
    send_wo(0)
    send_direct(0, "b")
    relayout(1)
    gather_finish(by_rows)
    bytes_wait(ga.at[pl.ds(0, DEV - 1)], s_gain.at[2])
    bytes_wait(gm.at[pl.ds(0, DEV - 1)], s_gain.at[3])

    def column_block(slot, carry):
        xcol[slot] = u[slot, :, mycols]
        return carry
    lax.fori_loop(0, DEV, column_block, 0)
    norm_all(ga, 0)

    def layer(l, carry):
        ld_d = pltpu.make_async_copy(wd_in.at[l], wd, l_sem.at[1])
        ld_d.start()
        bytes_wait(land_qkv.at[l, pl.ds(0, OTHER), :], rs_qkv.at[l])
        load_qkv(l)
        bytes_wait(wqkv, ld_sem.at[0])

        def qkv_block(i, carry):
            prod = jnp.dot(u[pl.ds(i * 2, 2)].reshape(2 * SEQ, DIM), wqkv[...], preferred_element_type=F32)
            cos, sin = cos_t[...], sin_t[...]
            for s in range(2):
                rows = slice(s * SEQ, (s + 1) * SEQ)
                for h in range(QH + 1):
                    head = prod[rows, h * HD:(h + 1) * HD]
                    rot = (head * cos + pltpu.roll(head, HD // 2, 1) * sin).astype(BF16)
                    if h < QH:
                        qb[i * 2 + s, pl.ds(h * SEQ, SEQ), :] = rot
                    else:
                        kb[i * 2 + s] = rot
                vb[i * 2 + s] = prod[rows, (QH + 1) * HD:].astype(BF16)
            return carry
        lax.fori_loop(0, DEV // 2, qkv_block, 0)

        def attend(s, carry):
            scores = lax.dot_general(qb[s], kb[s], (((1,), (1,)), ((), ())), preferred_element_type=F32) * HD ** -0.5
            row = lax.broadcasted_iota(jnp.int32, (QH * SEQ, SEQ), 0) % SEQ
            col = lax.broadcasted_iota(jnp.int32, (QH * SEQ, SEQ), 1)
            scores = jnp.where(row >= col, scores, -jnp.inf)
            e = jnp.exp(scores - jnp.max(scores, axis=-1, keepdims=True))
            probs = (e / jnp.sum(e, axis=-1, keepdims=True)).astype(BF16)
            o = jnp.dot(probs, vb[s], preferred_element_type=F32).astype(BF16)
            for h in range(QH):
                ob[s, :, h * HD:(h + 1) * HD] = o[h * SEQ:(h + 1) * SEQ]
            return carry
        lax.fori_loop(0, DEV, attend, 0)

        def after_exchange():
            for n in SPLIT:
                if n != AHEAD:
                    send_gu(l, n, "a")

            @pl.when(l == 0)
            def _():
                send_gu(l, AHEAD, "a")

            bytes_wait(land_wo.at[l], rs_wo.at[l])
            load_wo(l)
            bytes_wait(wo, l_sem.at[0])

        out_proj(l, after_exchange, lambda: None)

        gather_start(by_cols)
        gather_forward(by_cols)
        for which in ("a", "b"):
            send_gu(l, LAST, which)
        send_direct(l, "d")
        send_gu(l, LAST, "d")

        @pl.when(l + 1 < LAYERS)
        def _():
            send_qkv(l + 1)

        own_last(l)
        gather_finish(by_cols)
        norm_all(gm, l)
        group_arrives(l, 0)
        group_arrives(l, 1)

        def activate(prod, n, i):
            off, w = CHUNKS[n]
            gate = prod[:, :w].astype(BF16).astype(F32)
            up = prod[:, w:].astype(BF16).astype(F32)
            z = (gate * jax.nn.sigmoid(gate) * up).astype(BF16)
            zb[pl.ds(i * CHIPS, CHIPS), :, off:off + w] = z.reshape(CHIPS, SEQ, w)

        def mlp_group(g):
            chunks, slot = GROUPS[g]
            first, width = group_cols(g)
            bytes_wait(wgu.at[slot, :, pl.ds(0, width)], ld_sem.at[1 + g])

            def block(i, carry):
                rows = u[pl.ds(i * CHIPS, CHIPS)].reshape(CHIPS * SEQ, DIM)
                prod = jnp.dot(rows, wgu[slot, :, :width], preferred_element_type=F32)
                for n in chunks:
                    base = 2 * CHUNKS[n][0] - first
                    activate(prod[:, base:base + 2 * CHUNKS[n][1]], n, i)
                return carry
            lax.fori_loop(0, 2, block, 0)

        def last_term(i, k):
            depth = pl.ds(pl.multiple_of(k * PAIR, PAIR), PAIR)
            rows = u[pl.ds(i * CHIPS, CHIPS), :, depth].reshape(CHIPS * SEQ, PAIR)
            return jnp.dot(rows, wlast[depth, :], preferred_element_type=F32)

        def last_near(i, carry):
            lsum[i] = (last_term(i, chip) + last_term(i, chip_x)) + last_term(i, chip_y)
            return carry

        def last_block(i):
            activate(lsum[i] + last_term(i, chip_d), LAST, i)

        mlp_group(0)
        group_arrives(l, 2)
        mlp_group(1)
        mlp_group(2)
        group_arrives(l, 3)
        mlp_group(3)
        ld_d.wait()

        def before_last(i, carry):
            slots = pl.ds(i * CHIPS, CHIPS)
            z = zb[slots, :, :KPRE].reshape(CHIPS * SEQ, KPRE)
            for p in range(NP):
                prod = jnp.dot(z, wd[:KPRE, p * PW:(p + 1) * PW], preferred_element_type=F32)
                part[slots, :, p * PW:(p + 1) * PW] = prod.reshape(CHIPS, SEQ, PW)
            return carry
        lax.fori_loop(0, 2, before_last, 0)
        bytes_wait(wlast.at[pl.ds(0, OTHER - PAIR), :], rs_gu.at[l, LAST])
        bytes_wait(wlast.at[pl.ds(0, ROWS), :], ld_sem.at[1 + len(GROUPS)])
        lax.fori_loop(0, 2, last_near, 0)
        bytes_wait(wlast.at[pl.ds(0, PAIR), :], rs_gu.at[l, LAST + 1])

        @pl.when(l + 1 < LAYERS)
        def _():
            last_block(0)
            last_block(1)
            reduce_scatter(False, zb, wd, KPRE, None, lambda: send_gu(l + 1, 0))
            gather_start(by_cols)
            gather_forward(by_cols)
            send_wo(l + 1)
            send_gu(l + 1, AHEAD, "a")
            send_direct(l + 1, "b")
            gather_finish(by_cols)
            norm_all(ga, l + 1)

        @pl.when(l + 1 == LAYERS)
        def _():
            def residual(slot, carry):
                part[slot, :, mycols] = part[slot, :, mycols] + xcol[slot].astype(F32)
                return carry
            lax.fori_loop(0, DEV, residual, 0)
            last_block(1 - c)
            reduce_scatter(True, zb, wd, KPRE, lambda: last_block(c), lambda: None)

        bytes_wait(land_wo.at[l], ss_wo.at[l])
        bytes_wait(land_qkv.at[l, pl.ds(0, OTHER), :], ss_qkv.at[l])
        for n in range(NCH):
            bytes_wait(gu_bytes(l, n), ss_gu.at[l, n])
        return carry

    lax.fori_loop(0, LAYERS, layer, 0)
    bytes_wait(ga.at[pl.ds(0, DEV - 1)], s_gain.at[0])
    bytes_wait(gm.at[pl.ds(0, DEV - 1)], s_gain.at[1])


def solution(mesh):
    batch_spec = P(("dp", "fsdp"), None, None)
    gain_spec = P(None, "fsdp")
    proj_spec = P(None, "fsdp", None, None)
    mat_spec = P(None, "fsdp", None)
    cos, sin = rope_tables()

    def local_forward(hidden, attn_norm, w_q, w_k, w_v, w_o, mlp_norm, w_gate, w_up, w_down):
        hbm = pl.BlockSpec(memory_space=pltpu.HBM)
        vmem = pl.BlockSpec(memory_space=pltpu.VMEM)
        dma = pltpu.SemaphoreType.DMA
        out = pl.pallas_call(
            body,
            name="two_layers",
            out_shape=(pltpu.VMEM((SEQ, DIM), BF16),
                       jax.ShapeDtypeStruct((LAYERS, DEV, ROWS, QKV), BF16),
                       jax.ShapeDtypeStruct((LAYERS, DIM, QKV), BF16),
                       jax.ShapeDtypeStruct((LAYERS, DIM, 2 * FCOLS), BF16),
                       jax.ShapeDtypeStruct((LAYERS, ROWS, 2 * PAIR), BF16)),
            in_specs=[hbm] * 12,
            out_specs=(vmem, hbm, hbm, hbm, hbm),
            scratch_shapes=[
                pltpu.VMEM((2, RB, DEV * QH, HD), BF16),
                pltpu.VMEM((2, RB, DEV, HD), BF16),
                pltpu.VMEM((2, RB, DEV, HD), BF16),
                pltpu.VMEM((2, DEV, RB, QKV), BF16),
                pltpu.VMEM((DEV, SEQ, ROWS), BF16),
                pltpu.VMEM((DEV, SEQ, DIM), BF16),
                pltpu.VMEM((DEV, SEQ, DIM), F32),
                pltpu.VMEM((NP, CHIPS, 2, SEQ, ROWS), F32),
                pltpu.VMEM((NP, 2, 2, SEQ, ROWS), F32),
                pltpu.VMEM((NP, 2, SEQ, ROWS), F32),
                pltpu.VMEM((DIM, QKV), BF16),
                pltpu.VMEM((2 * ROWS, 2 * PAIR), BF16),
                pltpu.VMEM((FCOLS, DIM), BF16),
                pltpu.VMEM((2, DIM, WIDE), BF16),
                pltpu.VMEM((DIM, 2 * CHUNKS[LAST][1]), BF16),
                pltpu.VMEM((2, CHIPS * SEQ, 2 * CHUNKS[LAST][1]), F32),
                pltpu.VMEM((DEV, QH * SEQ, HD), BF16),
                pltpu.VMEM((DEV, SEQ, HD), BF16),
                pltpu.VMEM((DEV, SEQ, HD), BF16),
                pltpu.VMEM((DEV, SEQ, QCOLS), BF16),
                pltpu.VMEM((DEV, SEQ, QCOLS), BF16),
                pltpu.VMEM((DEV, SEQ, FCOLS), BF16),
                pltpu.VMEM((DEV, LAYERS, ROWS), BF16),
                pltpu.VMEM((DEV, LAYERS, ROWS), BF16),
                pltpu.VMEM((SEQ, HD), F32),
                pltpu.VMEM((SEQ, HD), F32),
                dma((LAYERS,)), dma((LAYERS,)), dma((LAYERS,)), dma((LAYERS,)), dma((2,)), dma((2,)), dma((LAYERS, NCH)), dma((LAYERS, NCH + 1)), dma((4,)), dma((7,)), dma((2 + len(GROUPS),)),
                dma((2, 3)), dma((2,)),
                dma((10,)), dma((10,)), dma((NP, 4)), dma((NP, 4)), dma((NP, 2)), dma((NP, 2)), dma((NP,)), dma((NP,)),
            ],
            compiler_params=pltpu.CompilerParams(collective_id=0, has_side_effects=True, vmem_limit_bytes=65_000_000),
        )(hidden[0], attn_norm, mlp_norm, cos, sin, w_q, w_k, w_v, w_o, w_gate, w_up, w_down)[0]
        return out[None]

    return jax.shard_map(local_forward, mesh=mesh, in_specs=(batch_spec, gain_spec, proj_spec, proj_spec, proj_spec, mat_spec, gain_spec, mat_spec, mat_spec, mat_spec), out_specs=batch_spec, check_vma=False)
```

time: 672 us -> 653 us (0.972)
  Pallas kernels: 671 us -> 651 us
    pallas_call x1, Pallas kernels: 671 us -> 651 us  [local_forward(): pl.pallas_call(body, name='two_layers', out_shape=(pltpu.VMEM((SEQ, DIM),...]
where the time goes in v4:
time: 653 us; the launch traced here: 652 us
  Pallas kernels  651 us (100%)
    pallas_call x1, Pallas kernels, local_forward(): pl.pallas_call(body, name='two_layers', out_shape=(pltpu.VMEM((SEQ, DIM),...  651 us

profile of v4, /device:TPU:0, one launch (start us, length us, event | category | flops | bytes accessed | tf_op | source)
XLA Modules:
  0.0 652.1 jit_solution(5012329777918268601)
XLA Ops:
  0.0 651.2 %two_layers.1 = (bf16[128,3072]{1,0:T(8,128)(2,1)S(1)}, bf16[2,8,384,640]{3,2,1,0:T(8,128)(2,1)}, bf16[2,3072,640]{2,1,0:T(8,128)(2,1)}, bf16[2,3072,2048]{2,1,0:T(8,128)(2,1)}, bf16[2,384,1536]{2,1,0:T(8,128)(2,1)}) custom-call(bf16[128,3072]{1,0:T(8,128)(2,1)} %bitcast.3, bf16[2,384]{1,0:T(2,128)(2,1)} %ga_in.1, bf16[2,384]{1,0:T(2,128)(2,1)} %gm_in.1, ...), custom_call_target="tpu_custom_call" | custom-call | tf_op jit(solution)/shard_map/two_layers/pallas_call | solution.py:617
  651.2 0.9 copy.14

commit v5 on v4

--- a/solution.py
+++ b/solution.py
@@ -34,7 +34,7 @@
 AHEAD = 3
 WIDE = 512
 SPLIT = (1, 2, 3, 4)
-KPRE = CHUNKS[LAST][0]
+KPRE = CHUNKS[LAST - 1][0]
 LAYERS = 2
 RB = 96
 NP = 4
@@ -514,7 +514,6 @@
         gather_finish(by_cols)
         norm_all(gm, l)
         group_arrives(l, 0)
-        group_arrives(l, 1)
 
         def activate(prod, n, i):
             off, w = CHUNKS[n]
@@ -550,11 +549,10 @@
             activate(lsum[i] + last_term(i, chip_d), LAST, i)
 
         mlp_group(0)
+        group_arrives(l, 1)
+        mlp_group(1)
         group_arrives(l, 2)
-        mlp_group(1)
         mlp_group(2)
-        group_arrives(l, 3)
-        mlp_group(3)
         ld_d.wait()
 
         def before_last(i, carry):
@@ -565,9 +563,11 @@
                 part[slots, :, p * PW:(p + 1) * PW] = prod.reshape(CHIPS, SEQ, PW)
             return carry
         lax.fori_loop(0, 2, before_last, 0)
+        group_arrives(l, 3)
         bytes_wait(wlast.at[pl.ds(0, OTHER - PAIR), :], rs_gu.at[l, LAST])
         bytes_wait(wlast.at[pl.ds(0, ROWS), :], ld_sem.at[1 + len(GROUPS)])
         lax.fori_loop(0, 2, last_near, 0)
+        mlp_group(3)
         bytes_wait(wlast.at[pl.ds(0, PAIR), :], rs_gu.at[l, LAST + 1])
 
         @pl.when(l + 1 < LAYERS)

time: 653 us -> 649 us (level)
  no operation moved by 1% of the time
where the time goes in v5:
time: 649 us; the launch traced here: 648 us
  Pallas kernels  647 us (100%)
    pallas_call x1, Pallas kernels, local_forward(): pl.pallas_call(body, name='two_layers', out_shape=(pltpu.VMEM((SEQ, DIM),...  647 us

profile of v5, /device:TPU:0, one launch (start us, length us, event | category | flops | bytes accessed | tf_op | source)
XLA Modules:
  0.0 648.4 jit_solution(652928871302527369)
XLA Ops:
  0.0 647.5 %two_layers.1 = (bf16[128,3072]{1,0:T(8,128)(2,1)S(1)}, bf16[2,8,384,640]{3,2,1,0:T(8,128)(2,1)}, bf16[2,3072,640]{2,1,0:T(8,128)(2,1)}, bf16[2,3072,2048]{2,1,0:T(8,128)(2,1)}, bf16[2,384,1536]{2,1,0:T(8,128)(2,1)}) custom-call(bf16[128,3072]{1,0:T(8,128)(2,1)} %bitcast.3, bf16[2,384]{1,0:T(2,128)(2,1)} %ga_in.1, bf16[2,384]{1,0:T(2,128)(2,1)} %gm_in.1, ...), custom_call_target="tpu_custom_call" | custom-call | tf_op jit(solution)/shard_map/two_layers/pallas_call | solution.py:617
  647.5 0.9 copy.14

commit v6 on v5

--- a/solution.py
+++ b/solution.py
@@ -369,10 +369,13 @@
             for p in both:
                 if rows_form:
                     products(p, other, (0, 1))
-                for k in (0, 1):
-                    if not rows_form:
-                        column_products(p, k)
-                    send_mate(p, k)
+                else:
+                    column_products(p, 0)
+                send_mate(p, 0)
+            for p in both:
+                if not rows_form:
+                    column_products(p, 1)
+                send_mate(p, 1)
             if pair == 0 and between is not None:
                 between()
             if rows_form:
@@ -421,9 +424,6 @@
         for n in SPLIT:
             send_gu(l, n, which)
 
-    for src, dst, k in ((ga_in, ga, 0), (gm_in, gm, 1)):
-        for f in flips:
-            remote(src, dst.at[me], s_gain.at[k], s_gain.at[2 + k], dev(*f)).start()
     send_gu(0, 0)
     starts = [pltpu.make_async_copy(src, dst, l_sem.at[2 + k]) for k, (src, dst) in enumerate(
         ((x_in, u.at[my_slot]), (ga_in, ga.at[me]), (gm_in, gm.at[me]), (cos_in, cos_t), (sin_in, sin_t)))]
@@ -432,6 +432,9 @@
     for cp in starts:
         cp.wait()
     gather_start(by_rows)
+    for src, dst, k in ((ga_in, ga, 0), (gm_in, gm, 1)):
+        for f in flips:
+            remote(src, dst.at[me], s_gain.at[k], s_gain.at[2 + k], dev(*f)).start()
     relayout(0)
     gather_forward(by_rows)
     send_qkv(0)

time: 649 us -> 648 us (level)
  no operation moved by 1% of the time
where the time goes in v6:
time: 648 us
  Pallas kernels  647 us (100%)
    pallas_call x1, Pallas kernels, local_forward(): pl.pallas_call(body, name='two_layers', out_shape=(pltpu.VMEM((SEQ, DIM),...  647 us

profile of v6, /device:TPU:0, one launch (start us, length us, event | category | flops | bytes accessed | tf_op | source)
XLA Modules:
  0.0 647.6 jit_solution(4114179085960259448)
XLA Ops:
  0.0 646.7 %two_layers.1 = (bf16[128,3072]{1,0:T(8,128)(2,1)S(1)}, bf16[2,8,384,640]{3,2,1,0:T(8,128)(2,1)}, bf16[2,3072,640]{2,1,0:T(8,128)(2,1)}, bf16[2,3072,2048]{2,1,0:T(8,128)(2,1)}, bf16[2,384,1536]{2,1,0:T(8,128)(2,1)}) custom-call(bf16[128,3072]{1,0:T(8,128)(2,1)} %bitcast.3, bf16[2,384]{1,0:T(2,128)(2,1)} %ga_in.1, bf16[2,384]{1,0:T(2,128)(2,1)} %gm_in.1, ...), custom_call_target="tpu_custom_call" | custom-call | tf_op jit(solution)/shard_map/two_layers/pallas_call | solution.py:620
  646.7 0.9 copy.14

commit v7 on v6

--- a/solution.py
+++ b/solution.py
@@ -31,7 +31,7 @@
 NCH = len(CHUNKS)
 LAST = NCH - 1
 GROUPS = (((1,), 0), ((2,), 1), ((0, 3), 0), ((4,), 1))
-AHEAD = 3
+AHEAD = (3, 4)
 WIDE = 512
 SPLIT = (1, 2, 3, 4)
 KPRE = CHUNKS[LAST - 1][0]
@@ -489,23 +489,23 @@
 
         def after_exchange():
             for n in SPLIT:
-                if n != AHEAD:
+                if n not in AHEAD:
                     send_gu(l, n, "a")
 
             @pl.when(l == 0)
             def _():
-                send_gu(l, AHEAD, "a")
+                for n in AHEAD:
+                    send_gu(l, n, "a")
 
             bytes_wait(land_wo.at[l], rs_wo.at[l])
             load_wo(l)
             bytes_wait(wo, l_sem.at[0])
 
-        out_proj(l, after_exchange, lambda: None)
+        out_proj(l, after_exchange, lambda: send_gu(l, LAST, "b"))
 
         gather_start(by_cols)
         gather_forward(by_cols)
-        for which in ("a", "b"):
-            send_gu(l, LAST, which)
+        send_gu(l, LAST, "a")
         send_direct(l, "d")
         send_gu(l, LAST, "d")
 
@@ -581,7 +581,8 @@
             gather_start(by_cols)
             gather_forward(by_cols)
             send_wo(l + 1)
-            send_gu(l + 1, AHEAD, "a")
+            for n in AHEAD:
+                send_gu(l + 1, n, "a")
             send_direct(l + 1, "b")
             gather_finish(by_cols)
             norm_all(ga, l + 1)

time: 648 us -> 648 us (level)
  no operation moved by 1% of the time
where the time goes in v7:
time: 648 us
  Pallas kernels  647 us (100%)
    pallas_call x1, Pallas kernels, local_forward(): pl.pallas_call(body, name='two_layers', out_shape=(pltpu.VMEM((SEQ, DIM),...  647 us

profile of v7, /device:TPU:0, one launch (start us, length us, event | category | flops | bytes accessed | tf_op | source)
XLA Modules:
  0.0 647.6 jit_solution(16742090001688163164)
XLA Ops:
  0.0 646.7 %two_layers.1 = (bf16[128,3072]{1,0:T(8,128)(2,1)S(1)}, bf16[2,8,384,640]{3,2,1,0:T(8,128)(2,1)}, bf16[2,3072,640]{2,1,0:T(8,128)(2,1)}, bf16[2,3072,2048]{2,1,0:T(8,128)(2,1)}, bf16[2,384,1536]{2,1,0:T(8,128)(2,1)}) custom-call(bf16[128,3072]{1,0:T(8,128)(2,1)} %bitcast.3, bf16[2,384]{1,0:T(2,128)(2,1)} %ga_in.1, bf16[2,384]{1,0:T(2,128)(2,1)} %gm_in.1, ...), custom_call_target="tpu_custom_call" | custom-call | tf_op jit(solution)/shard_map/two_layers/pallas_call | solution.py:621
  646.7 0.9 copy.14

commit v8 on v7

--- a/solution.py
+++ b/solution.py
@@ -401,7 +401,7 @@
             fold(p, 2, r1.at[p, 0])
             pieces(p, order[p % 2][2], own, r2.at[p], r2_s.at[p], r2_r.at[p], second[p % 2])
         for p in range(NP):
-            if p == NP // 2:
+            if p == 0:
                 then()
             unit(mt_r.at[p, 3])
             unit(r1_r.at[p, 1])

time: 648 us -> 648 us (level)
  no operation moved by 1% of the time
where the time goes in v8:
time: 648 us; the launch traced here: 647 us
  Pallas kernels  646 us (100%)
    pallas_call x1, Pallas kernels, local_forward(): pl.pallas_call(body, name='two_layers', out_shape=(pltpu.VMEM((SEQ, DIM),...  646 us

profile of v8, /device:TPU:0, one launch (start us, length us, event | category | flops | bytes accessed | tf_op | source)
XLA Modules:
  0.0 647.2 jit_solution(1072596057505841466)
XLA Ops:
  0.0 646.3 %two_layers.1 = (bf16[128,3072]{1,0:T(8,128)(2,1)S(1)}, bf16[2,8,384,640]{3,2,1,0:T(8,128)(2,1)}, bf16[2,3072,640]{2,1,0:T(8,128)(2,1)}, bf16[2,3072,2048]{2,1,0:T(8,128)(2,1)}, bf16[2,384,1536]{2,1,0:T(8,128)(2,1)}) custom-call(bf16[128,3072]{1,0:T(8,128)(2,1)} %bitcast.3, bf16[2,384]{1,0:T(2,128)(2,1)} %ga_in.1, bf16[2,384]{1,0:T(2,128)(2,1)} %gm_in.1, ...), custom_call_target="tpu_custom_call" | custom-call | tf_op jit(solution)/shard_map/two_layers/pallas_call | solution.py:621
  646.3 0.9 copy.14
